TPU v7x, 128 devices: a whole 4x4x4 slice. The times are simulated.
128 devices in a mesh: ctx: 16 (over y, x), tp: 8 (over z, core).
Axes of the slice: x: 4, y: 4, z: 4, core: 2. Of those that a mesh axis runs over, the one named last changes fastest.
Arguments:
- hidden: bfloat16 [8, 8192], P(None, 'ctx'), may hold values from -4.8 to 4.8, as said below
- norm_gains: bfloat16 [4, 8192], P(None, 'ctx'), may hold values from 0.5 to 1.5
- w_query: bfloat16 [4, 8192, 8192], P(None, 'ctx', 'tp'), may hold values from -0.0625 to 0.0625
- w_key: bfloat16 [4, 8192, 1024], P(None, 'ctx', 'tp'), may hold values from -0.125 to 0.125
- w_value: bfloat16 [4, 8192, 1024], P(None, 'ctx', 'tp'), may hold values from -0.125 to 0.125
- w_out: bfloat16 [4, 8192, 8192], P(None, 'tp', 'ctx'), may hold values from -0.0625 to 0.0625
- key_cache: bfloat16 [4, 8, 8, 2048, 128], P(None, None, 'tp', 'ctx'), may hold values from -9 to 9
- value_cache: bfloat16 [4, 8, 8, 2048, 128], P(None, None, 'tp', 'ctx'), may hold values from -6 to 6
- lengths: int32 [8], replicated, may hold values from 1 to 2048, 8200 in all
Outputs:
- updated: float32 [8, 8192], P(None, 'ctx')
Inputs may be any that keep to these rules, and one draw needn't show every extreme that they name: Each sequence has lengths[b] valid cache positions 0 .. lengths[b] - 1, between 1 and 2048; the longest sequence has exactly 2048; the new token sits at position lengths[b]. `hidden`: activations of order 0.2; in each block of 512 consecutive features one sequence, chosen at random, has entries four times larger.
All inputs are finite; a program needn't handle non-finite values.
Results may differ from a plain program's by a relative error of at most 0.02.
Values sent between devices are 32-bit elements.
A program may use at most 64 MiB of HBM per device.

v0:
```python
import functools
import math

import jax
import jax.numpy as jnp
from jax import lax
from jax.experimental import pallas as pl
from jax.experimental.pallas import tpu as pltpu
from jax.sharding import PartitionSpec as P

mask_fill = -1e30
norm_eps = 1e-05
rope_base = 500000.0
MESH = pl.DeviceIdType.MESH


def kernel(dims, hidden_ref, gains_ref, lengths_ref, wq_h, wk_h, wv_h, wo_h, kc_h, vc_h, out_ref,
           wq, wk, wv, wo, kc, vc, gain, bias, cosine, sine, qp, qr, kvp, kvr, qf, qown, otmp, stmp,
           op, orr, cf, tps, tpr, w_sem, s_sem, r_sem, ts_sem, tr_sem):
    n, tn, layers, batch, feat, total, heads, kvl, hd, span = dims
    group = heads // kvl
    hpo = max(1, heads // n)
    owners = heads // hpo
    f32, bf16 = jnp.float32, jnp.bfloat16
    pieces = tps.shape[0]
    piece = feat // pieces
    scale = 1.0 / math.sqrt(hd)
    me = lax.axis_index("ctx")
    mt = lax.axis_index("tp")
    weights = ((wq_h, wq), (wk_h, wk), (wv_h, wv), (kc_h, kc), (vc_h, vc), (wo_h, wo))

    def load(index, layer):
        source, target = weights[index]
        return pltpu.make_async_copy(source.at[layer], target.at[layer], w_sem.at[index, layer])

    for index in range(len(weights)):
        load(index, 0).start()

    peers = [lax.rem(me + r, n) for r in range(1, n)]
    tpeers = [lax.rem(mt + r, tn) for r in range(1, tn)]
    barrier = pltpu.get_barrier_semaphore()
    for p in peers:
        pl.semaphore_signal(barrier, inc=1, device_id={"ctx": p}, device_id_type=MESH)
    for p in tpeers:
        pl.semaphore_signal(barrier, inc=1, device_id={"tp": p}, device_id_type=MESH)

    row = lax.broadcasted_iota(jnp.int32, (batch, hd), 0)
    lane = lax.broadcasted_iota(jnp.int32, (batch, hd), 1)
    times = jnp.zeros((batch, hd), jnp.int32)
    slot = lax.broadcasted_iota(jnp.int32, (heads, span), 1) + me * span
    for b in range(batch):
        times = jnp.where(row == b, lengths_ref[b], times)
        bias[b * heads:(b + 1) * heads, :] = jnp.where(slot < lengths_ref[b], 0.0, mask_fill)
    half = hd // 2
    low = lane < half
    exponent = jnp.where(low, lane, lane - half).astype(f32) * (2.0 / hd)
    angle = times.astype(f32) * jnp.exp(-exponent * math.log(rope_base))
    cosine[...] = jnp.cos(angle)
    sine[...] = jnp.where(low, -jnp.sin(angle), jnp.sin(angle))
    for l in range(layers):
        gain[l] = jnp.broadcast_to(gains_ref[l:l + 1, :].astype(f32), (batch, feat))
    out_ref[...] = hidden_ref[...].astype(f32)

    pl.semaphore_wait(barrier, n - 1 + tn - 1)

    def rotate(u):
        return u * cosine[...] + pltpu.roll(u, half, 1) * sine[...]

    def rounded(u):
        return u.astype(bf16).astype(f32)

    def send(kind, r, source, target):
        return pltpu.make_async_remote_copy(
            src_ref=source, dst_ref=target, send_sem=s_sem.at[kind, r - 1],
            recv_sem=r_sem.at[kind, r - 1], device_id={"ctx": peers[r - 1]}, device_id_type=MESH)

    order = sorted(range(1, n), key=lambda r: (-min(r, n - r), r))
    mine = lax.rem(me, owners)
    my_kv = (mine * hpo) // group
    rows = hpo * batch
    my_rows = pl.ds(pl.multiple_of(me * rows, rows), rows)
    width = hpo * hd

    def layer_step(l, carry):
        stream = out_ref[...]
        scaled = (stream * gain[l]).astype(bf16)
        squares = stream * stream
        fold = squares[:, 0:hd]
        for c in range(1, feat // hd):
            fold = fold + squares[:, c * hd:(c + 1) * hd]
        load(0, l).wait()

        @pl.when(l + 1 < layers)
        def _():
            for index in range(len(weights)):
                load(index, l + 1).start()

        q = jnp.dot(scaled, wq[l], preferred_element_type=f32)
        for i in range(owners):
            qp[i, :, 0:width] = q[:, i * width:(i + 1) * width]
            qp[i, :, width:width + hd] = fold
        qs = []
        for r in order:
            c = send(0, r, qp.at[lax.rem(peers[r - 1], owners)], qr.at[r - 1])
            c.start()
            qs.append(c)
        load(1, l).wait()
        load(2, l).wait()
        k = jnp.dot(scaled, wk[l], preferred_element_type=f32)
        v = jnp.dot(scaled, wv[l], preferred_element_type=f32)
        for j in range(kvl):
            kvp[j, :, 0:hd] = k[:, j * hd:(j + 1) * hd]
            kvp[j, :, hd:2 * hd] = v[:, j * hd:(j + 1) * hd]
        ks = []
        for r in order:
            owner = lax.rem(peers[r - 1], owners)
            c = send(1, r, kvp.at[(owner * hpo) // group], kvr.at[r - 1])
            c.start()
            ks.append(c)
        for c in qs:
            c.wait_recv()
        whole = qp[mine]
        for r in range(1, n):
            whole = whole + qr[r - 1]
        inverse = lax.rsqrt(jnp.sum(whole[:, width:width + hd], axis=1, keepdims=True) / total + norm_eps)
        for t in range(hpo):
            u = rotate(whole[:, t * hd:(t + 1) * hd] * inverse)
            qown[t] = rounded(u)
            qf[pl.ds(pl.multiple_of(me * rows + t * batch, batch), batch), :] = u
        gs = []
        for r in order:
            c = send(2, r, qf.at[my_rows], qf.at[my_rows])
            c.start()
            gs.append(c)
        for c in ks:
            c.wait_recv()
        kv = kvp[my_kv]
        for r in range(1, n):
            kv = kv + kvr[r - 1]
        new_key = rounded(rotate(kv[:, 0:hd] * inverse))
        new_value = rounded(kv[:, hd:2 * hd] * inverse)
        own = [jnp.sum(qown[t] * new_key, axis=1, keepdims=True) * scale for t in range(hpo)]
        load(3, l).wait()
        load(4, l).wait()
        for c in gs:
            c.wait_recv()
        scores = []
        for b in range(batch):
            qb = qf[pl.ds(b, heads, stride=batch), :].astype(bf16)
            for j in range(kvl):
                scores.append(lax.dot_general(
                    qb[j * group:(j + 1) * group], kc[l, b, j], (((1,), (1,)), ((), ())),
                    preferred_element_type=f32))
        masked = jnp.concatenate(scores, axis=0) * scale + bias[...]
        top = jnp.max(masked, axis=1, keepdims=True)
        weight = jnp.exp(masked - top)
        weight_sum = jnp.sum(weight, axis=1, keepdims=True)
        narrow = weight.astype(bf16)
        lanes = lax.broadcasted_iota(jnp.int32, (batch * heads, hd), 1)
        stmp[...] = jnp.where(lax.rem(lanes, 2) == 0, top, weight_sum)
        for b in range(batch):
            for j in range(kvl):
                at = b * heads + j * group
                otmp[at:at + group, :] = jnp.dot(narrow[at:at + group], vc[l, b, j], preferred_element_type=f32)
        for c in qs + ks + gs:
            c.wait_send()
        for i in range(owners):
            stat = None
            for t in range(hpo):
                h = i * hpo + t
                op[i, t * batch:(t + 1) * batch, :] = otmp[pl.ds(h, batch, stride=heads), :]
                tile = stmp[pl.ds(h, batch, stride=heads), :]
                stat = tile if stat is None else jnp.where(lane < 2 * t, stat, tile)
            op[i, rows:rows + batch, :] = stat
        os_ = []
        for r in order:
            c = send(3, r, op.at[lax.rem(peers[r - 1], owners)], orr.at[r - 1])
            c.start()
            os_.append(c)
        for c in os_:
            c.wait_recv()
        parts = [op[mine]] + [orr[r - 1] for r in range(1, n)]
        for t in range(hpo):
            tops = [part[rows:rows + batch, 2 * t:2 * t + 1] for part in parts]
            sums = [part[rows:rows + batch, 2 * t + 1:2 * t + 2] for part in parts]
            largest = own[t]
            for x in tops:
                largest = jnp.maximum(largest, x)
            fresh = jnp.exp(own[t] - largest)
            numerator = rounded(fresh) * new_value
            denominator = fresh
            for x, s, part in zip(tops, sums, parts):
                factor = jnp.exp(x - largest)
                denominator = denominator + s * factor
                numerator = numerator + part[t * batch:(t + 1) * batch, :] * factor
            cf[pl.ds(pl.multiple_of(me, 1), 1), :, t * hd:(t + 1) * hd] = (numerator / denominator)[None]
        cs = []
        for r in order:
            c = send(4, r, cf.at[me], cf.at[me])
            c.start()
            cs.append(c)
        load(5, l).wait()
        for c in cs:
            c.wait_recv()
        context = jnp.concatenate([cf[i] for i in range(owners)], axis=1).astype(bf16)
        odd = lax.rem(l, 2)
        ts = []
        for g in range(pieces):
            cut = slice(g * piece, (g + 1) * piece)
            tps[g] = jnp.dot(context, wo[l, :, cut], preferred_element_type=f32)
            for r in range(1, tn):
                c = pltpu.make_async_remote_copy(
                    src_ref=tps.at[g], dst_ref=tpr.at[odd, g, r - 1], send_sem=ts_sem.at[g, r - 1],
                    recv_sem=tr_sem.at[odd, g, r - 1], device_id={"tp": tpeers[r - 1]}, device_id_type=MESH)
                c.start()
                ts.append(c)
        for c in os_ + cs:
            c.wait_send()
        for g in range(pieces):
            cut = slice(g * piece, (g + 1) * piece)
            moved = out_ref[:, cut] + tps[g]
            for r in range(1, tn):
                ts[g * (tn - 1) + r - 1].wait_recv()
                moved = moved + tpr[odd, g, r - 1]
            out_ref[:, cut] = moved
        for c in ts:
            c.wait_send()
        return carry

    lax.fori_loop(0, layers, layer_step, 0)


def shards(sizes, hidden, norm_gains, w_query, w_key, w_value, w_out, key_cache, value_cache, lengths):
    n, tn = sizes
    layers, feat, columns = w_query.shape
    batch = hidden.shape[0]
    _, _, kvl, span, hd = key_cache.shape
    heads = columns // hd
    hpo = max(1, heads // n)
    owners = heads // hpo
    dims = (n, tn, layers, batch, feat, feat * n, heads, kvl, hd, span)
    pieces = 2
    f32 = jnp.float32
    vmem = pl.BlockSpec(memory_space=pltpu.VMEM)
    far = pl.BlockSpec(memory_space=pl.ANY)

    def like(array):
        return pltpu.VMEM(array.shape, array.dtype)

    return pl.pallas_call(
        functools.partial(kernel, dims),
        out_shape=jax.ShapeDtypeStruct((batch, feat), f32),
        in_specs=[vmem, vmem, pl.BlockSpec(memory_space=pltpu.SMEM)] + [far] * 6,
        out_specs=vmem,
        scratch_shapes=[
            like(w_query), like(w_key), like(w_value), like(w_out), like(key_cache), like(value_cache),
            pltpu.VMEM((layers, batch, feat), f32),
            pltpu.VMEM((batch * heads, span), f32),
            pltpu.VMEM((batch, hd), f32),
            pltpu.VMEM((batch, hd), f32),
            pltpu.VMEM((owners, batch, hpo * hd + hd), f32),
            pltpu.VMEM((n - 1, batch, hpo * hd + hd), f32),
            pltpu.VMEM((kvl, batch, 2 * hd), f32),
            pltpu.VMEM((n - 1, batch, 2 * hd), f32),
            pltpu.VMEM((n * hpo * batch, hd), f32),
            pltpu.VMEM((hpo, batch, hd), f32),
            pltpu.VMEM((batch * heads, hd), f32),
            pltpu.VMEM((batch * heads, hd), f32),
            pltpu.VMEM((owners, hpo * batch + batch, hd), f32),
            pltpu.VMEM((n - 1, hpo * batch + batch, hd), f32),
            pltpu.VMEM((n, batch, hpo * hd), f32),
            pltpu.VMEM((pieces, batch, feat // pieces), f32),
            pltpu.VMEM((2, pieces, tn - 1, batch, feat // pieces), f32),
            pltpu.SemaphoreType.DMA((6, layers)),
            pltpu.SemaphoreType.DMA((5, n - 1)),
            pltpu.SemaphoreType.DMA((5, n - 1)),
            pltpu.SemaphoreType.DMA((pieces, tn - 1)),
            pltpu.SemaphoreType.DMA((2, pieces, tn - 1)),
        ],
        compiler_params=pltpu.CompilerParams(
            collective_id=0, has_side_effects=True, vmem_limit_bytes=60 * 1024 * 1024),
    )(hidden, norm_gains, lengths, w_query, w_key, w_value, w_out, key_cache, value_cache)


def solution(mesh):
    sizes = (mesh.shape["ctx"], mesh.shape["tp"])
    return jax.shard_map(
        functools.partial(shards, sizes),
        mesh=mesh,
        in_specs=(
            P(None, "ctx"),
            P(None, "ctx"),
            P(None, "ctx", "tp"),
            P(None, "ctx", "tp"),
            P(None, "ctx", "tp"),
            P(None, "tp", "ctx"),
            P(None, None, "tp", "ctx", None),
            P(None, None, "tp", "ctx", None),
            P(),
        ),
        out_specs=P(None, "ctx"),
        check_vma=False,
    )
```

profile of v0, /device:TPU:1, one launch (start us, length us, event | category | flops | bytes accessed | tf_op | source)
XLA Modules:
  0.0 114.2 jit_solution(4958639103253842456)
XLA Ops:
  0.0 112.8 %shard_map.91 = f32[8,512]{1,0:T(8,128)} custom-call(bf16[8,512]{1,0:T(8,128)(2,1)} %hidden_ref.1, bf16[4,512]{1,0:T(4,128)(2,1)} %gains_ref.1, s32[8]{0:T(128)} %lengths_ref.1, bf16[4,512,1024]{2,1,0:T(8,128)(2,1)} %wq_h.1, bf16[4,512,128]{2,1,0:T(8,128)(2,1)} %wk_h.1, bf16[4,512,128]{2,1,0:T(8,128)(2,1)} %wv_h.1, bf16[4,1024,512]{2,1,0:T(8,128)(2,1)} %wo_h.1, ...), custom_call_target="tpu_custom_call" | custom-call | tf_op jit(solution)/shard_map/pallas_call | solution.py:250
  112.8 1.3 %copy.11 = f32[8,512]{1,0:T(8,128)} copy(f32[8,512]{1,0:T(8,128)} %shard_map.91) | data formatting | bytes 32768
where the time goes:
time: 114 us
  Pallas kernels  113 us (99%)
  local copies, waits for them, and re-layouts  1.32 us (1%)
    pallas_call x1, Pallas kernels, shards(): pl.pallas_call(functools.partial(kernel, dims), out_shape=jax.ShapeDtypeS...  113 us

commit v1 on v0

v1 whole, which is shorter than its diff:
```python
import functools
import math

import jax
import jax.numpy as jnp
from jax import lax
from jax.experimental import pallas as pl
from jax.experimental.pallas import tpu as pltpu
from jax.sharding import PartitionSpec as P

mask_fill = -1e30
norm_eps = 1e-05
rope_base = 500000.0
MESH = pl.DeviceIdType.MESH
QROWS = 11


def kernel(dims, hidden_ref, gains_ref, lengths_ref, wq_h, wk_h, wv_h, wo_h, kc_h, vc_h, out_ref,
           wq, wk, wv, wo, kc, vc, gain, bias, cosine, sine, qs, qr, kst, vst, krv, vrv, kb, vb,
           orr, cm, tps, tpr, w_sem, qs_sem, qr_sem, os_sem, or_sem, ts_sem, tr_sem, hs_sem, hr_sem):
    n, tn, side, layers, batch, feat, total, heads, hd, span = dims
    f32, bf16 = jnp.float32, jnp.bfloat16
    pieces = tps.shape[0]
    piece = feat // pieces
    scale = 1.0 / math.sqrt(hd)
    me = lax.axis_index("ctx")
    mt = lax.axis_index("tp")
    y, x = me // side, lax.rem(me, side)
    z, core = mt // 2, lax.rem(mt, 2)
    zn = tn // 2
    weights = ((kc_h, kc), (vc_h, vc), (wq_h, wq), (wk_h, wk), (wv_h, wv), (wo_h, wo))
    KC, VC, WQ, WK, WV, WO = range(6)

    def load(index, layer):
        source, target = weights[index]
        return pltpu.make_async_copy(source.at[layer], target.at[layer], w_sem.at[index, layer])

    for index in range(len(weights)):
        load(index, 0).start()

    def hops(step, size):
        return min(step, size - step)

    offsets = [(dy, dx) for dy in range(side) for dx in range(side) if (dy, dx) != (0, 0)]
    offsets.sort(key=lambda o: -(hops(o[0], side) + hops(o[1], side)))
    peers = []
    for dy, dx in offsets:
        py, px = lax.rem(y + dy, side), lax.rem(x + dx, side)
        peers.append((py * side + px, py, px))
    toffsets = [(dz, dc) for dz in range(zn) for dc in range(2) if (dz, dc) != (0, 0)]
    toffsets.sort(key=lambda o: -(2 * hops(o[0], zn) + o[1]))
    tpeers = [lax.rem(z + dz, zn) * 2 + lax.rem(core + dc, 2) for dz, dc in toffsets]

    barrier = pltpu.get_barrier_semaphore()
    for p, _, _ in peers:
        pl.semaphore_signal(barrier, inc=1, device_id={"ctx": p}, device_id_type=MESH)
    for p in tpeers:
        pl.semaphore_signal(barrier, inc=1, device_id={"tp": p}, device_id_type=MESH)

    half = hd // 2
    lane = lax.broadcasted_iota(jnp.int32, (heads, hd), 1)
    low = lane < half
    mine = (x, side + y)
    slot = lax.broadcasted_iota(jnp.int32, (heads, side * span), 1)
    block = slot // span
    positions = (y * side * span + slot, (block * side + x) * span + lax.rem(slot, span))
    exponent = jnp.where(low, lane, lane - half).astype(f32) * (2.0 / hd)
    frequency = jnp.exp(-exponent * math.log(rope_base))
    for g in range(2):
        size = lengths_ref[mine[g]]
        bias[g] = jnp.where(positions[g] < size, 0.0, mask_fill)
        angle = jnp.full((heads, hd), size, jnp.int32).astype(f32) * frequency
        cosine[g] = jnp.cos(angle)
        sine[g] = jnp.where(low, -jnp.sin(angle), jnp.sin(angle))
    for l in range(layers):
        gain[l] = jnp.broadcast_to(gains_ref[l:l + 1, :].astype(f32), (batch, feat))
    out_ref[...] = hidden_ref[...].astype(f32)
    own_mask = jnp.where(jnp.full((heads, 1), y, jnp.int32) == jnp.full((heads, 1), x, jnp.int32), 0.0, mask_fill)

    def ship(l):
        copies = []
        for r in range(1, side):
            px, py = lax.rem(x + r, side), lax.rem(y + r, side)
            for i, (source, target) in enumerate(((kst, krv), (vst, vrv))):
                copies.append(pltpu.make_async_remote_copy(
                    src_ref=source.at[l, px], dst_ref=target.at[l, 0, x],
                    send_sem=hs_sem.at[l, i, 0, r - 1], recv_sem=hr_sem.at[l, i, 0, r - 1],
                    device_id={"ctx": y * side + px}, device_id_type=MESH))
                copies.append(pltpu.make_async_remote_copy(
                    src_ref=source.at[l, side + py], dst_ref=target.at[l, 1, y],
                    send_sem=hs_sem.at[l, i, 1, r - 1], recv_sem=hr_sem.at[l, i, 1, r - 1],
                    device_id={"ctx": py * side + x}, device_id_type=MESH))
        return copies

    def stage(l):
        load(KC, l).wait()
        load(VC, l).wait()
        for source, staged, held in ((kc, kst, krv), (vc, vst, vrv)):
            for b in range(batch):
                staged[l, b] = source[l, b, 0].astype(f32)
            held[l, 0, x] = source[l, mine[0], 0].astype(f32)
            held[l, 1, y] = source[l, mine[1], 0].astype(f32)

    stage(0)
    pl.semaphore_wait(barrier, n - 1 + tn - 1)
    for c in ship(0):
        c.start()

    def rotate(u, g):
        return u * cosine[g] + pltpu.roll(u, half, 1) * sine[g]

    def rounded(u):
        return u.astype(bf16).astype(f32)

    def layer_step(l, carry):
        stream = out_ref[...]
        scaled = (stream * gain[l]).astype(bf16)
        squares = jnp.sum(stream * stream, axis=1, keepdims=True)
        load(WQ, l).wait()
        load(WK, l).wait()
        load(WV, l).wait()

        @pl.when(l + 1 < layers)
        def _():
            for index in range(len(weights)):
                load(index, l + 1).start()

        def put(row, tile):
            qs[pl.ds(row, batch, stride=16), :] = tile

        put(heads, jnp.dot(scaled, wk[l], preferred_element_type=f32))
        put(heads + 1, jnp.dot(scaled, wv[l], preferred_element_type=f32))
        put(heads + 2, jnp.broadcast_to(squares, (batch, hd)))
        q = jnp.dot(scaled, wq[l], preferred_element_type=f32)
        for h in range(heads):
            put(h, q[:, h * hd:(h + 1) * hd])
        qc = []
        for k, (p, py, px) in enumerate(peers):
            for g, b in ((0, px), (1, side + py)):
                c = pltpu.make_async_remote_copy(
                    src_ref=qs.at[pl.ds(pl.multiple_of(b * 16, 16), QROWS)], dst_ref=qr.at[k, g, pl.ds(0, QROWS)],
                    send_sem=qs_sem.at[k, g], recv_sem=qr_sem.at[k, g],
                    device_id={"ctx": p}, device_id_type=MESH)
                c.start()
                qc.append(c)

        for c in ship(l):
            c.wait()
        for g in range(2):
            kb[g] = krv[l, g].reshape(side * span, hd).astype(bf16)
            vb[g] = vrv[l, g].reshape(side * span, hd).astype(bf16)

        for c in qc:
            c.wait_recv()
        stats = []
        for g in range(2):
            at = pl.multiple_of(mine[g] * 16, 16)
            whole = qs[pl.ds(at, heads), :]
            rest = qs[pl.ds(pl.multiple_of(at + 8, 8), QROWS - heads), :]
            for k in range(n - 1):
                whole = whole + qr[k, g, 0:heads]
                rest = rest + qr[k, g, heads:QROWS]
            inverse = lax.rsqrt(rest[2:3] / total + norm_eps)
            query = rounded(rotate(whole * inverse, g))
            new_key = rounded(rotate(jnp.broadcast_to(rest[0:1] * inverse, (heads, hd)), g))
            new_value = rounded(rest[1:2] * inverse)
            score = lax.dot_general(query.astype(bf16), kb[g], (((1,), (1,)), ((), ())), preferred_element_type=f32)
            own = jnp.sum(query * new_key, axis=1, keepdims=True) * scale + own_mask
            masked = score * scale + bias[g]
            top = jnp.maximum(jnp.max(masked, axis=1, keepdims=True), own)
            weight = jnp.exp(masked - top)
            fresh = jnp.exp(own - top)
            denominator = jnp.sum(weight, axis=1, keepdims=True) + fresh
            numerator = jnp.dot(weight.astype(bf16), vb[g], preferred_element_type=f32) + rounded(fresh) * new_value
            orr[me, g * heads:(g + 1) * heads, :] = numerator / denominator
            stats.append(top + jnp.log(denominator))
        orr[me, 2 * heads:3 * heads, :] = jnp.where(low, stats[0], stats[1])
        oc = []
        for k, (p, _, _) in enumerate(peers):
            c = pltpu.make_async_remote_copy(
                src_ref=orr.at[me], dst_ref=orr.at[me], send_sem=os_sem.at[k], recv_sem=or_sem.at[k],
                device_id={"ctx": p}, device_id_type=MESH)
            c.start()
            oc.append(c)

        @pl.when(l + 1 < layers)
        def _():
            stage(l + 1)

        load(WO, l).wait()
        for c in qc:
            c.wait_send()
        for c in oc:
            c.wait_recv()

        @pl.when(l + 1 < layers)
        def _():
            for c in ship(l + 1):
                c.start()

        logs = [orr[c, 2 * heads:3 * heads, :] for c in range(n)]
        groups = [[[r * side + b for r in range(side)] for b in range(side)],
                  [[b * side + r for r in range(side)] for b in range(side)]]

        def over(values, op):
            return [[functools.reduce(op, [values[c] for c in group]) for group in part] for part in groups]

        def split(pair, c):
            return jnp.where(low, pair[0][c % side], pair[1][c // side])

        largest = over(logs, jnp.maximum)
        factors = [jnp.exp(logs[c] - split(largest, c)) for c in range(n)]
        sums = over(factors, jnp.add)
        inverses = [[1.0 / s for s in part] for part in sums]
        factors = [factors[c] * split(inverses, c) for c in range(n)]
        swapped = [pltpu.roll(f, half, 1) for f in factors]
        for g in range(2):
            for b, group in enumerate(groups[g]):
                merged = None
                for c in group:
                    factor = jnp.where(low, factors[c], swapped[c]) if g == 0 else jnp.where(low, swapped[c], factors[c])
                    term = orr[c, g * heads:(g + 1) * heads, :] * factor
                    merged = term if merged is None else merged + term
                at = (g * side + b) * heads
                cm[at:at + heads, :] = merged
        context = jnp.concatenate([cm[pl.ds(h, batch, stride=heads), :] for h in range(heads)], axis=1).astype(bf16)
        odd = lax.rem(l, 2)
        ts = []
        for i in range(pieces):
            cut = slice(i * piece, (i + 1) * piece)
            tps[i] = jnp.dot(context, wo[l, :, cut], preferred_element_type=f32)
            for k, p in enumerate(tpeers):
                c = pltpu.make_async_remote_copy(
                    src_ref=tps.at[i], dst_ref=tpr.at[odd, i, k], send_sem=ts_sem.at[i, k],
                    recv_sem=tr_sem.at[odd, i, k], device_id={"tp": p}, device_id_type=MESH)
                c.start()
                ts.append(c)
        for c in oc:
            c.wait_send()
        for i in range(pieces):
            cut = slice(i * piece, (i + 1) * piece)
            moved = out_ref[:, cut] + tps[i]
            for k in range(tn - 1):
                ts[i * (tn - 1) + k].wait_recv()
                moved = moved + tpr[odd, i, k]
            out_ref[:, cut] = moved
        for c in ts:
            c.wait_send()
        return carry

    lax.fori_loop(0, layers, layer_step, 0)


def shards(sizes, hidden, norm_gains, w_query, w_key, w_value, w_out, key_cache, value_cache, lengths):
    n, tn = sizes
    layers, feat, columns = w_query.shape
    batch = hidden.shape[0]
    _, _, _, span, hd = key_cache.shape
    heads = columns // hd
    side = math.isqrt(n)
    dims = (n, tn, side, layers, batch, feat, feat * n, heads, hd, span)
    pieces = 2
    f32, bf16 = jnp.float32, jnp.bfloat16
    vmem = pl.BlockSpec(memory_space=pltpu.VMEM)
    far = pl.BlockSpec(memory_space=pl.ANY)

    def like(array):
        return pltpu.VMEM(array.shape, array.dtype)

    dma = pltpu.SemaphoreType.DMA
    return pl.pallas_call(
        functools.partial(kernel, dims),
        out_shape=jax.ShapeDtypeStruct((batch, feat), f32),
        in_specs=[vmem, vmem, pl.BlockSpec(memory_space=pltpu.SMEM)] + [far] * 6,
        out_specs=vmem,
        scratch_shapes=[
            like(w_query), like(w_key), like(w_value), like(w_out), like(key_cache), like(value_cache),
            pltpu.VMEM((layers, batch, feat), f32),
            pltpu.VMEM((2, heads, side * span), f32),
            pltpu.VMEM((2, heads, hd), f32),
            pltpu.VMEM((2, heads, hd), f32),
            pltpu.VMEM((batch * 16, hd), f32),
            pltpu.VMEM((n - 1, 2, 16, hd), f32),
            pltpu.VMEM((layers, batch, span, hd), f32),
            pltpu.VMEM((layers, batch, span, hd), f32),
            pltpu.VMEM((layers, 2, side, span, hd), f32),
            pltpu.VMEM((layers, 2, side, span, hd), f32),
            pltpu.VMEM((2, side * span, hd), bf16),
            pltpu.VMEM((2, side * span, hd), bf16),
            pltpu.VMEM((n, 3 * heads, hd), f32),
            pltpu.VMEM((batch * heads, hd), f32),
            pltpu.VMEM((pieces, batch, feat // pieces), f32),
            pltpu.VMEM((2, pieces, tn - 1, batch, feat // pieces), f32),
            dma((6, layers)),
            dma((n - 1, 2)), dma((n - 1, 2)),
            dma((n - 1,)), dma((n - 1,)),
            dma((pieces, tn - 1)), dma((2, pieces, tn - 1)),
            dma((layers, 2, 2, side - 1)), dma((layers, 2, 2, side - 1)),
        ],
        compiler_params=pltpu.CompilerParams(
            collective_id=0, has_side_effects=True, vmem_limit_bytes=60 * 1024 * 1024),
    )(hidden, norm_gains, lengths, w_query, w_key, w_value, w_out, key_cache, value_cache)


def solution(mesh):
    sizes = (mesh.shape["ctx"], mesh.shape["tp"])
    return jax.shard_map(
        functools.partial(shards, sizes),
        mesh=mesh,
        in_specs=(
            P(None, "ctx"),
            P(None, "ctx"),
            P(None, "ctx", "tp"),
            P(None, "ctx", "tp"),
            P(None, "ctx", "tp"),
            P(None, "tp", "ctx"),
            P(None, None, "tp", "ctx", None),
            P(None, None, "tp", "ctx", None),
            P(),
        ),
        out_specs=P(None, "ctx"),
        check_vma=False,
    )
```

time: 114 us -> 81.3 us (0.71)
  Pallas kernels: 113 us -> 79.7 us
    pallas_call x1, Pallas kernels: 113 us -> 79.7 us  [shards(): pl.pallas_call(functools.partial(kernel, dims), out_shape=jax.ShapeDtypeS...]
where the time goes in v1:
time: 81.3 us; the launch traced here: 81.1 us
  Pallas kernels  79.7 us (98%)
  local copies, waits for them, and re-layouts  1.32 us (2%)
    pallas_call x1, Pallas kernels, shards(): pl.pallas_call(functools.partial(kernel, dims), out_shape=jax.ShapeDtypeS...  79.7 us

profile of v1, /device:TPU:1, one launch (start us, length us, event | category | flops | bytes accessed | tf_op | source)
XLA Modules:
  0.0 81.1 jit_solution(739018392353289794)
XLA Ops:
  0.0 79.7 %shard_map.91 = f32[8,512]{1,0:T(8,128)} custom-call(bf16[8,512]{1,0:T(8,128)(2,1)} %hidden_ref.1, bf16[4,512]{1,0:T(4,128)(2,1)} %gains_ref.1, s32[8]{0:T(128)} %lengths_ref.1, bf16[4,512,1024]{2,1,0:T(8,128)(2,1)} %wq_h.1, bf16[4,512,128]{2,1,0:T(8,128)(2,1)} %wk_h.1, bf16[4,512,128]{2,1,0:T(8,128)(2,1)} %wv_h.1, bf16[4,1024,512]{2,1,0:T(8,128)(2,1)} %wo_h.1, ...), custom_call_target="tpu_custom_call" | custom-call | tf_op jit(solution)/shard_map/pallas_call | solution.py:271
  79.8 1.3 %copy.11 = f32[8,512]{1,0:T(8,128)} copy(f32[8,512]{1,0:T(8,128)} %shard_map.91) | data formatting | bytes 32768

commit v2 on v1

--- a/solution.py
+++ b/solution.py
@@ -15,9 +15,9 @@
 QROWS = 11
 
 
-def kernel(dims, hidden_ref, gains_ref, lengths_ref, wq_h, wk_h, wv_h, wo_h, kc_h, vc_h, out_ref,
-           wq, wk, wv, wo, kc, vc, gain, bias, cosine, sine, qs, qr, kst, vst, krv, vrv, kb, vb,
-           orr, cm, tps, tpr, w_sem, qs_sem, qr_sem, os_sem, or_sem, ts_sem, tr_sem, hs_sem, hr_sem):
+def kernel(dims, hidden_h, gains_h, lengths_h, wq_h, wk_h, wv_h, wo_h, kc_h, vc_h, out_ref,
+           hidden_ref, gains_ref, lengths_ref, wq, wk, wv, wo, kc, vc, gain, bias, cosine, sine, qs, qr, kst, vst, krv, vrv, kb, vb,
+           orr, cm, tps, tpr, w_sem, qs_sem, qr_sem, os_sem, or_sem, ts_sem, tr_sem, hs_sem, hr_sem, small_sem, ready):
     n, tn, side, layers, batch, feat, total, heads, hd, span = dims
     f32, bf16 = jnp.float32, jnp.bfloat16
     pieces = tps.shape[0]
@@ -35,9 +35,6 @@
         source, target = weights[index]
         return pltpu.make_async_copy(source.at[layer], target.at[layer], w_sem.at[index, layer])
 
-    for index in range(len(weights)):
-        load(index, 0).start()
-
     def hops(step, size):
         return min(step, size - step)
 
@@ -51,11 +48,24 @@
     toffsets.sort(key=lambda o: -(2 * hops(o[0], zn) + o[1]))
     tpeers = [lax.rem(z + dz, zn) * 2 + lax.rem(core + dc, 2) for dz, dc in toffsets]
 
+    column = [lax.rem(y + r, side) * side + x for r in range(1, side)]
+    row = [y * side + lax.rem(x + r, side) for r in range(1, side)]
     barrier = pltpu.get_barrier_semaphore()
-    for p, _, _ in peers:
+    for p in row + column:
         pl.semaphore_signal(barrier, inc=1, device_id={"ctx": p}, device_id_type=MESH)
     for p in tpeers:
         pl.semaphore_signal(barrier, inc=1, device_id={"tp": p}, device_id_type=MESH)
+
+    smalls = [pltpu.make_async_copy(source, target, small_sem.at[i]) for i, (source, target) in enumerate(
+        ((hidden_h, hidden_ref), (gains_h, gains_ref), (lengths_h, lengths_ref)))]
+    for index in (KC, VC):
+        load(index, 0).start()
+    for c in smalls:
+        c.start()
+    for index in (WQ, WK, WV, WO):
+        load(index, 0).start()
+    for c in smalls:
+        c.wait()
 
     half = hd // 2
     lane = lax.broadcasted_iota(jnp.int32, (heads, hd), 1)
@@ -102,9 +112,12 @@
             held[l, 1, y] = source[l, mine[1], 0].astype(f32)
 
     stage(0)
-    pl.semaphore_wait(barrier, n - 1 + tn - 1)
+    pl.semaphore_wait(barrier, len(row) + len(column) + len(tpeers))
+    for p in column:
+        pl.semaphore_signal(ready, inc=1, device_id={"ctx": p}, device_id_type=MESH)
     for c in ship(0):
         c.start()
+    pl.semaphore_wait(ready, len(column))
 
     def rotate(u, g):
         return u * cosine[g] + pltpu.roll(u, half, 1) * sine[g]
@@ -193,11 +206,6 @@
         for c in oc:
             c.wait_recv()
 
-        @pl.when(l + 1 < layers)
-        def _():
-            for c in ship(l + 1):
-                c.start()
-
         logs = [orr[c, 2 * heads:3 * heads, :] for c in range(n)]
         groups = [[[r * side + b for r in range(side)] for b in range(side)],
                   [[b * side + r for r in range(side)] for b in range(side)]]
@@ -235,6 +243,11 @@
                     recv_sem=tr_sem.at[odd, i, k], device_id={"tp": p}, device_id_type=MESH)
                 c.start()
                 ts.append(c)
+        @pl.when(l + 1 < layers)
+        def _():
+            for c in ship(l + 1):
+                c.start()
+
         for c in oc:
             c.wait_send()
         for i in range(pieces):
@@ -270,10 +283,11 @@
     dma = pltpu.SemaphoreType.DMA
     return pl.pallas_call(
         functools.partial(kernel, dims),
-        out_shape=jax.ShapeDtypeStruct((batch, feat), f32),
-        in_specs=[vmem, vmem, pl.BlockSpec(memory_space=pltpu.SMEM)] + [far] * 6,
+        out_shape=pltpu.VMEM((batch, feat), f32),
+        in_specs=[far] * 9,
         out_specs=vmem,
         scratch_shapes=[
+            like(hidden), like(norm_gains), pltpu.SMEM(lengths.shape, lengths.dtype),
             like(w_query), like(w_key), like(w_value), like(w_out), like(key_cache), like(value_cache),
             pltpu.VMEM((layers, batch, feat), f32),
             pltpu.VMEM((2, heads, side * span), f32),
@@ -296,6 +310,7 @@
             dma((n - 1,)), dma((n - 1,)),
             dma((pieces, tn - 1)), dma((2, pieces, tn - 1)),
             dma((layers, 2, 2, side - 1)), dma((layers, 2, 2, side - 1)),
+            dma((3,)), pltpu.SemaphoreType.REGULAR,
         ],
         compiler_params=pltpu.CompilerParams(
             collective_id=0, has_side_effects=True, vmem_limit_bytes=60 * 1024 * 1024),

time: 81.3 us -> 79.1 us (0.973)
  Pallas kernels: 79.7 us -> 78.3 us
    pallas_call x1, Pallas kernels: 79.7 us -> 78.3 us  [shards(): pl.pallas_call(functools.partial(kernel, dims), out_shape=pltpu.VMEM((bat...]
where the time goes in v2:
time: 79.1 us; the launch traced here: 78.9 us
  Pallas kernels  78.3 us (99%)
    pallas_call x1, Pallas kernels, shards(): pl.pallas_call(functools.partial(kernel, dims), out_shape=pltpu.VMEM((bat...  78.3 us

profile of v2, /device:TPU:1, one launch (start us, length us, event | category | flops | bytes accessed | tf_op | source)
XLA Modules:
  0.0 78.9 jit_solution(16901015214345679392)
XLA Ops:
  0.0 78.3 %shard_map.91 = f32[8,512]{1,0:T(8,128)S(1)} custom-call(bf16[8,512]{1,0:T(8,128)(2,1)} %hidden_h.1, bf16[4,512]{1,0:T(4,128)(2,1)} %gains_h.1, s32[8]{0:T(128)} %lengths_h.1, bf16[4,512,1024]{2,1,0:T(8,128)(2,1)} %wq_h.1, bf16[4,512,128]{2,1,0:T(8,128)(2,1)} %wk_h.1, bf16[4,512,128]{2,1,0:T(8,128)(2,1)} %wv_h.1, bf16[4,1024,512]{2,1,0:T(8,128)(2,1)} %wo_h.1, ...), custom_call_target="tpu_custom_call" | custom-call | tf_op jit(solution)/shard_map/pallas_call | solution.py:284
  78.3 0.6 copy.11

commit v3 on v2

--- a/solution.py
+++ b/solution.py
@@ -89,7 +89,7 @@
 
     def ship(l):
         copies = []
-        for r in range(1, side):
+        for r in (2, 1, 3):
             px, py = lax.rem(x + r, side), lax.rem(y + r, side)
             for i, (source, target) in enumerate(((kst, krv), (vst, vrv))):
                 copies.append(pltpu.make_async_remote_copy(
@@ -206,6 +206,11 @@
         for c in oc:
             c.wait_recv()
 
+        @pl.when(l + 1 < layers)
+        def _():
+            for c in ship(l + 1):
+                c.start()
+
         logs = [orr[c, 2 * heads:3 * heads, :] for c in range(n)]
         groups = [[[r * side + b for r in range(side)] for b in range(side)],
                   [[b * side + r for r in range(side)] for b in range(side)]]
@@ -243,11 +248,6 @@
                     recv_sem=tr_sem.at[odd, i, k], device_id={"tp": p}, device_id_type=MESH)
                 c.start()
                 ts.append(c)
-        @pl.when(l + 1 < layers)
-        def _():
-            for c in ship(l + 1):
-                c.start()
-
         for c in oc:
             c.wait_send()
         for i in range(pieces):

time: 79.1 us -> 77.2 us (0.976)
  Pallas kernels: 78.3 us -> 76.5 us
    pallas_call x1, Pallas kernels: 78.3 us -> 76.5 us  [shards(): pl.pallas_call(functools.partial(kernel, dims), out_shape=pltpu.VMEM((bat...]
where the time goes in v3:
time: 77.2 us; the launch traced here: 77.1 us
  Pallas kernels  76.5 us (99%)
    pallas_call x1, Pallas kernels, shards(): pl.pallas_call(functools.partial(kernel, dims), out_shape=pltpu.VMEM((bat...  76.5 us

profile of v3, /device:TPU:1, one launch (start us, length us, event | category | flops | bytes accessed | tf_op | source)
XLA Modules:
  0.0 77.1 jit_solution(3085913625680293875)
XLA Ops:
  0.0 76.5 %shard_map.91 = f32[8,512]{1,0:T(8,128)S(1)} custom-call(bf16[8,512]{1,0:T(8,128)(2,1)} %hidden_h.1, bf16[4,512]{1,0:T(4,128)(2,1)} %gains_h.1, s32[8]{0:T(128)} %lengths_h.1, bf16[4,512,1024]{2,1,0:T(8,128)(2,1)} %wq_h.1, bf16[4,512,128]{2,1,0:T(8,128)(2,1)} %wk_h.1, bf16[4,512,128]{2,1,0:T(8,128)(2,1)} %wv_h.1, bf16[4,1024,512]{2,1,0:T(8,128)(2,1)} %wo_h.1, ...), custom_call_target="tpu_custom_call" | custom-call | tf_op jit(solution)/shard_map/pallas_call | solution.py:284
  76.5 0.6 copy.11

commit v4 on v3

--- a/solution.py
+++ b/solution.py
@@ -12,12 +12,12 @@
 norm_eps = 1e-05
 rope_base = 500000.0
 MESH = pl.DeviceIdType.MESH
-QROWS = 11
+QROWS = 9
 
 
 def kernel(dims, hidden_h, gains_h, lengths_h, wq_h, wk_h, wv_h, wo_h, kc_h, vc_h, out_ref,
-           hidden_ref, gains_ref, lengths_ref, wq, wk, wv, wo, kc, vc, gain, bias, cosine, sine, qs, qr, kst, vst, krv, vrv, kb, vb,
-           orr, cm, tps, tpr, w_sem, qs_sem, qr_sem, os_sem, or_sem, ts_sem, tr_sem, hs_sem, hr_sem, small_sem, ready):
+           hidden_ref, gains_ref, lengths_ref, wq, wk, wv, wo, kc, vc, gain, bias, cosine, sine, qs, qr, ks, kr, fresh_sum, kst, vst, krv, vrv, kb, vb,
+           orr, cm, tps, tpr, w_sem, qs_sem, qr_sem, ks_sem, kr_sem, os_sem, or_sem, ts_sem, tr_sem, hs_sem, hr_sem, small_sem, ready):
     n, tn, side, layers, batch, feat, total, heads, hd, span = dims
     f32, bf16 = jnp.float32, jnp.bfloat16
     pieces = tps.shape[0]
@@ -111,6 +111,12 @@
             held[l, 0, x] = source[l, mine[0], 0].astype(f32)
             held[l, 1, y] = source[l, mine[1], 0].astype(f32)
 
+    def fresh_copy(d):
+        return pltpu.make_async_remote_copy(
+            src_ref=ks.at[pl.ds(8 * d, 4)], dst_ref=kr.at[me], send_sem=ks_sem.at[d], recv_sem=kr_sem,
+            device_id={"ctx": d * side + d}, device_id_type=MESH)
+
+    fresh_sum[...] = jnp.zeros_like(fresh_sum)
     stage(0)
     pl.semaphore_wait(barrier, len(row) + len(column) + len(tpeers))
     for p in column:
@@ -141,9 +147,16 @@
         def put(row, tile):
             qs[pl.ds(row, batch, stride=16), :] = tile
 
-        put(heads, jnp.dot(scaled, wk[l], preferred_element_type=f32))
-        put(heads + 1, jnp.dot(scaled, wv[l], preferred_element_type=f32))
-        put(heads + 2, jnp.broadcast_to(squares, (batch, hd)))
+        for i, w in enumerate((wk, wv)):
+            kv = jnp.dot(scaled, w[l], preferred_element_type=f32)
+            for g in range(2):
+                ks[pl.ds(2 * g + i, side, stride=8), :] = kv[g * side:(g + 1) * side]
+        for d in range(side):
+            @pl.when(me != d * side + d)
+            def _():
+                fresh_copy(d).start()
+
+        put(heads, jnp.broadcast_to(squares, (batch, hd)))
         q = jnp.dot(scaled, wq[l], preferred_element_type=f32)
         for h in range(heads):
             put(h, q[:, h * hd:(h + 1) * hd])
@@ -156,12 +169,17 @@
                     device_id={"ctx": p}, device_id_type=MESH)
                 c.start()
                 qc.append(c)
-
         for c in ship(l):
             c.wait()
         for g in range(2):
             kb[g] = krv[l, g].reshape(side * span, hd).astype(bf16)
             vb[g] = vrv[l, g].reshape(side * span, hd).astype(bf16)
+
+        @pl.when(y == x)
+        def _():
+            kr[me] = ks[pl.ds(pl.multiple_of(8 * x, 8), 4), :]
+            pltpu.make_async_copy(kr.at[pl.ds(0, n - 1)], kr.at[pl.ds(0, n - 1)], kr_sem).wait()
+            fresh_sum[...] = functools.reduce(jnp.add, [kr[c] for c in range(n)])
 
         for c in qc:
             c.wait_recv()
@@ -169,15 +187,15 @@
         for g in range(2):
             at = pl.multiple_of(mine[g] * 16, 16)
             whole = qs[pl.ds(at, heads), :]
-            rest = qs[pl.ds(pl.multiple_of(at + 8, 8), QROWS - heads), :]
+            square = qs[pl.ds(pl.multiple_of(at + 8, 8), 1), :]
             for k in range(n - 1):
                 whole = whole + qr[k, g, 0:heads]
-                rest = rest + qr[k, g, heads:QROWS]
-            inverse = lax.rsqrt(rest[2:3] / total + norm_eps)
+                square = square + qr[k, g, heads:QROWS]
+            inverse = lax.rsqrt(square / total + norm_eps)
             query = rounded(rotate(whole * inverse, g))
-            new_key = rounded(rotate(jnp.broadcast_to(rest[0:1] * inverse, (heads, hd)), g))
-            new_value = rounded(rest[1:2] * inverse)
             score = lax.dot_general(query.astype(bf16), kb[g], (((1,), (1,)), ((), ())), preferred_element_type=f32)
+            new_key = rounded(rotate(jnp.broadcast_to(fresh_sum[2 * g:2 * g + 1] * inverse, (heads, hd)), g))
+            new_value = rounded(fresh_sum[2 * g + 1:2 * g + 2] * inverse)
             own = jnp.sum(query * new_key, axis=1, keepdims=True) * scale + own_mask
             masked = score * scale + bias[g]
             top = jnp.maximum(jnp.max(masked, axis=1, keepdims=True), own)
@@ -203,6 +221,10 @@
         load(WO, l).wait()
         for c in qc:
             c.wait_send()
+        for d in range(side):
+            @pl.when(me != d * side + d)
+            def _():
+                fresh_copy(d).wait_send()
         for c in oc:
             c.wait_recv()
 
@@ -272,7 +294,7 @@
     heads = columns // hd
     side = math.isqrt(n)
     dims = (n, tn, side, layers, batch, feat, feat * n, heads, hd, span)
-    pieces = 2
+    pieces = 1
     f32, bf16 = jnp.float32, jnp.bfloat16
     vmem = pl.BlockSpec(memory_space=pltpu.VMEM)
     far = pl.BlockSpec(memory_space=pl.ANY)
@@ -295,6 +317,9 @@
             pltpu.VMEM((2, heads, hd), f32),
             pltpu.VMEM((batch * 16, hd), f32),
             pltpu.VMEM((n - 1, 2, 16, hd), f32),
+            pltpu.VMEM((side * 8, hd), f32),
+            pltpu.VMEM((n, 4, hd), f32),
+            pltpu.VMEM((4, hd), f32),
             pltpu.VMEM((layers, batch, span, hd), f32),
             pltpu.VMEM((layers, batch, span, hd), f32),
             pltpu.VMEM((layers, 2, side, span, hd), f32),
@@ -307,6 +332,7 @@
             pltpu.VMEM((2, pieces, tn - 1, batch, feat // pieces), f32),
             dma((6, layers)),
             dma((n - 1, 2)), dma((n - 1, 2)),
+            dma((side,)), dma(()),
             dma((n - 1,)), dma((n - 1,)),
             dma((pieces, tn - 1)), dma((2, pieces, tn - 1)),
             dma((layers, 2, 2, side - 1)), dma((layers, 2, 2, side - 1)),

time: 77.2 us -> 75.9 us (0.983)
  Pallas kernels: 76.5 us -> 75.2 us
    pallas_call x1, Pallas kernels: 76.5 us -> 75.2 us  [shards(): pl.pallas_call(functools.partial(kernel, dims), out_shape=pltpu.VMEM((bat...]
where the time goes in v4:
time: 75.9 us; the launch traced here: 75.8 us
  Pallas kernels  75.2 us (99%)
    pallas_call x1, Pallas kernels, shards(): pl.pallas_call(functools.partial(kernel, dims), out_shape=pltpu.VMEM((bat...  75.2 us

profile of v4, /device:TPU:1, one launch (start us, length us, event | category | flops | bytes accessed | tf_op | source)
XLA Modules:
  0.0 75.8 jit_solution(6833707169998240905)
XLA Ops:
  0.0 75.2 %shard_map.91 = f32[8,512]{1,0:T(8,128)S(1)} custom-call(bf16[8,512]{1,0:T(8,128)(2,1)} %hidden_h.1, bf16[4,512]{1,0:T(4,128)(2,1)} %gains_h.1, s32[8]{0:T(128)} %lengths_h.1, bf16[4,512,1024]{2,1,0:T(8,128)(2,1)} %wq_h.1, bf16[4,512,128]{2,1,0:T(8,128)(2,1)} %wk_h.1, bf16[4,512,128]{2,1,0:T(8,128)(2,1)} %wv_h.1, bf16[4,1024,512]{2,1,0:T(8,128)(2,1)} %wo_h.1, ...), custom_call_target="tpu_custom_call" | custom-call | tf_op jit(solution)/shard_map/pallas_call | solution.py:306
  75.2 0.6 copy.11

commit v5 on v4

--- a/solution.py
+++ b/solution.py
@@ -17,7 +17,7 @@
 
 def kernel(dims, hidden_h, gains_h, lengths_h, wq_h, wk_h, wv_h, wo_h, kc_h, vc_h, out_ref,
            hidden_ref, gains_ref, lengths_ref, wq, wk, wv, wo, kc, vc, gain, bias, cosine, sine, qs, qr, ks, kr, fresh_sum, kst, vst, krv, vrv, kb, vb,
-           orr, cm, tps, tpr, w_sem, qs_sem, qr_sem, ks_sem, kr_sem, os_sem, or_sem, ts_sem, tr_sem, hs_sem, hr_sem, small_sem, ready):
+           orr, od, cm, tps, tpr, w_sem, qs_sem, qr_sem, ks_sem, kr_sem, os_sem, or_sem, ts_sem, tr_sem, hs_sem, hr_sem, small_sem, ready):
     n, tn, side, layers, batch, feat, total, heads, hd, span = dims
     f32, bf16 = jnp.float32, jnp.bfloat16
     pieces = tps.shape[0]
@@ -51,8 +51,10 @@
     column = [lax.rem(y + r, side) * side + x for r in range(1, side)]
     row = [y * side + lax.rem(x + r, side) for r in range(1, side)]
     barrier = pltpu.get_barrier_semaphore()
+    cores = (2 * z, 2 * z + 1)
     for p in row + column:
-        pl.semaphore_signal(barrier, inc=1, device_id={"ctx": p}, device_id_type=MESH)
+        for t in cores:
+            pl.semaphore_signal(barrier, inc=1, device_id={"ctx": p, "tp": t}, device_id_type=MESH)
     for p in tpeers:
         pl.semaphore_signal(barrier, inc=1, device_id={"tp": p}, device_id_type=MESH)
 
@@ -87,20 +89,32 @@
     out_ref[...] = hidden_ref[...].astype(f32)
     own_mask = jnp.where(jnp.full((heads, 1), y, jnp.int32) == jnp.full((heads, 1), x, jnp.int32), 0.0, mask_fill)
 
-    def ship(l):
+    def ship(l, rounds):
         copies = []
-        for r in (2, 1, 3):
+        for r in rounds:
             px, py = lax.rem(x + r, side), lax.rem(y + r, side)
             for i, (source, target) in enumerate(((kst, krv), (vst, vrv))):
                 copies.append(pltpu.make_async_remote_copy(
-                    src_ref=source.at[l, px], dst_ref=target.at[l, 0, x],
-                    send_sem=hs_sem.at[l, i, 0, r - 1], recv_sem=hr_sem.at[l, i, 0, r - 1],
-                    device_id={"ctx": y * side + px}, device_id_type=MESH))
+                    src_ref=source.at[l, px], dst_ref=target.at[l, core, x],
+                    send_sem=hs_sem.at[l, i], recv_sem=hr_sem.at[l, core, i],
+                    device_id={"ctx": y * side + px, "tp": cores[1]}, device_id_type=MESH))
                 copies.append(pltpu.make_async_remote_copy(
-                    src_ref=source.at[l, side + py], dst_ref=target.at[l, 1, y],
-                    send_sem=hs_sem.at[l, i, 1, r - 1], recv_sem=hr_sem.at[l, i, 1, r - 1],
-                    device_id={"ctx": py * side + x}, device_id_type=MESH))
+                    src_ref=source.at[l, side + py], dst_ref=target.at[l, core, side + y],
+                    send_sem=hs_sem.at[l, i], recv_sem=hr_sem.at[l, core, i],
+                    device_id={"ctx": py * side + x, "tp": cores[1]}, device_id_type=MESH))
         return copies
+
+    def ship_start(l):
+        for c in ship(l, (2, 1, 3)):
+            c.start()
+
+        @pl.when(core == 0)
+        def _():
+            for c in ship(l, (0,)):
+                c.start()
+
+    def taken(ref, sem):
+        pltpu.make_async_copy(ref, ref, sem).wait()
 
     def stage(l):
         load(KC, l).wait()
@@ -108,28 +122,92 @@
         for source, staged, held in ((kc, kst, krv), (vc, vst, vrv)):
             for b in range(batch):
                 staged[l, b] = source[l, b, 0].astype(f32)
-            held[l, 0, x] = source[l, mine[0], 0].astype(f32)
-            held[l, 1, y] = source[l, mine[1], 0].astype(f32)
+
+            @pl.when(core == 1)
+            def _():
+                held[l, 1, x] = source[l, mine[0], 0].astype(f32)
+                held[l, 1, side + y] = source[l, mine[1], 0].astype(f32)
 
     def fresh_copy(d):
         return pltpu.make_async_remote_copy(
-            src_ref=ks.at[pl.ds(8 * d, 4)], dst_ref=kr.at[me], send_sem=ks_sem.at[d], recv_sem=kr_sem,
-            device_id={"ctx": d * side + d}, device_id_type=MESH)
+            src_ref=ks.at[pl.ds(8 * d, 4)], dst_ref=kr.at[core, me], send_sem=ks_sem.at[d], recv_sem=kr_sem.at[core],
+            device_id={"ctx": d * side + d, "tp": cores[1]}, device_id_type=MESH)
+
+    def fresh_sends(act):
+        for d in range(side):
+            @pl.when(jnp.logical_or(core == 0, me != d * side + d))
+            def _():
+                act(fresh_copy(d))
+
+    places = peers + [(me, y, x)]
+    far_chips = range(n - 1)
+
+    def q_copies(k):
+        p, py, px = places[k]
+        return [pltpu.make_async_remote_copy(
+            src_ref=qs.at[pl.ds(pl.multiple_of(b * 16, 16), QROWS)], dst_ref=qr.at[core, k, g, pl.ds(0, QROWS)],
+            send_sem=qs_sem.at[k, g], recv_sem=qr_sem.at[core, k, g],
+            device_id={"ctx": p, "tp": cores[1]}, device_id_type=MESH) for g, b in ((0, px), (1, side + py))]
+
+    def q_arrivals(h):
+        for k in range(n - h):
+            for g in range(2):
+                taken(qr.at[h, k, g, pl.ds(0, QROWS)], qr_sem.at[h, k, g])
+
+    def o_copy(h, k):
+        return pltpu.make_async_remote_copy(
+            src_ref=orr.at[me] if h else od, dst_ref=orr.at[me], send_sem=os_sem.at[h, k], recv_sem=or_sem.at[k],
+            device_id={"ctx": places[k][0], "tp": cores[h]}, device_id_type=MESH)
 
     fresh_sum[...] = jnp.zeros_like(fresh_sum)
     stage(0)
-    pl.semaphore_wait(barrier, len(row) + len(column) + len(tpeers))
+    pl.semaphore_wait(barrier, 2 * len(row) + 2 * len(column) + len(tpeers))
     for p in column:
-        pl.semaphore_signal(ready, inc=1, device_id={"ctx": p}, device_id_type=MESH)
-    for c in ship(0):
-        c.start()
-    pl.semaphore_wait(ready, len(column))
+        for t in cores:
+            pl.semaphore_signal(ready, inc=1, device_id={"ctx": p, "tp": t}, device_id_type=MESH)
+    ship_start(0)
+    pl.semaphore_wait(ready, 2 * len(column))
 
     def rotate(u, g):
         return u * cosine[g] + pltpu.roll(u, half, 1) * sine[g]
 
     def rounded(u):
         return u.astype(bf16).astype(f32)
+
+    def attend(h):
+        stats = []
+        for g in range(2):
+            whole, square = qr[h, 0, g, 0:heads], qr[h, 0, g, heads:QROWS]
+            for k in range(1, n - h):
+                whole = whole + qr[h, k, g, 0:heads]
+                square = square + qr[h, k, g, heads:QROWS]
+            if h:
+                at = pl.multiple_of(mine[g] * 16, 16)
+                whole = whole + qs[pl.ds(at, heads), :]
+                square = square + qs[pl.ds(pl.multiple_of(at + 8, 8), 1), :]
+            inverse = lax.rsqrt(square / total + norm_eps)
+            query = rounded(rotate(whole * inverse, g))
+            score = lax.dot_general(
+                query.astype(bf16), kb[h, g], (((1,), (1,)), ((), ())), preferred_element_type=f32)
+            new_key = fresh_sum[h, 2 * g:2 * g + 1] * inverse
+            new_key = rounded(rotate(jnp.broadcast_to(new_key, (heads, hd)), g))
+            new_value = rounded(fresh_sum[h, 2 * g + 1:2 * g + 2] * inverse)
+            own = jnp.sum(query * new_key, axis=1, keepdims=True) * scale + own_mask
+            masked = score * scale + bias[g]
+            top = jnp.maximum(jnp.max(masked, axis=1, keepdims=True), own)
+            weight = jnp.exp(masked - top)
+            fresh = jnp.exp(own - top)
+            denominator = jnp.sum(weight, axis=1, keepdims=True) + fresh
+            numerator = jnp.dot(weight.astype(bf16), vb[h, g], preferred_element_type=f32) + rounded(fresh) * new_value
+            if h:
+                orr[me, g * heads:(g + 1) * heads, :] = numerator / denominator
+            else:
+                od[g * heads:(g + 1) * heads, :] = numerator / denominator
+            stats.append(top + jnp.log(denominator))
+        if h:
+            orr[me, 2 * heads:3 * heads, :] = jnp.where(low, stats[0], stats[1])
+        else:
+            od[2 * heads:3 * heads, :] = jnp.where(low, stats[0], stats[1])
 
     def layer_step(l, carry):
         stream = out_ref[...]
@@ -151,87 +229,70 @@
             kv = jnp.dot(scaled, w[l], preferred_element_type=f32)
             for g in range(2):
                 ks[pl.ds(2 * g + i, side, stride=8), :] = kv[g * side:(g + 1) * side]
-        for d in range(side):
-            @pl.when(me != d * side + d)
-            def _():
-                fresh_copy(d).start()
-
+        fresh_sends(lambda c: c.start())
         put(heads, jnp.broadcast_to(squares, (batch, hd)))
         q = jnp.dot(scaled, wq[l], preferred_element_type=f32)
         for h in range(heads):
             put(h, q[:, h * hd:(h + 1) * hd])
-        qc = []
-        for k, (p, py, px) in enumerate(peers):
-            for g, b in ((0, px), (1, side + py)):
-                c = pltpu.make_async_remote_copy(
-                    src_ref=qs.at[pl.ds(pl.multiple_of(b * 16, 16), QROWS)], dst_ref=qr.at[k, g, pl.ds(0, QROWS)],
-                    send_sem=qs_sem.at[k, g], recv_sem=qr_sem.at[k, g],
-                    device_id={"ctx": p}, device_id_type=MESH)
+        for k in far_chips:
+            for c in q_copies(k):
                 c.start()
-                qc.append(c)
-        for c in ship(l):
-            c.wait()
-        for g in range(2):
-            kb[g] = krv[l, g].reshape(side * span, hd).astype(bf16)
-            vb[g] = vrv[l, g].reshape(side * span, hd).astype(bf16)
-
-        @pl.when(y == x)
-        def _():
-            kr[me] = ks[pl.ds(pl.multiple_of(8 * x, 8), 4), :]
-            pltpu.make_async_copy(kr.at[pl.ds(0, n - 1)], kr.at[pl.ds(0, n - 1)], kr_sem).wait()
-            fresh_sum[...] = functools.reduce(jnp.add, [kr[c] for c in range(n)])
-
-        for c in qc:
-            c.wait_recv()
-        stats = []
-        for g in range(2):
-            at = pl.multiple_of(mine[g] * 16, 16)
-            whole = qs[pl.ds(at, heads), :]
-            square = qs[pl.ds(pl.multiple_of(at + 8, 8), 1), :]
-            for k in range(n - 1):
-                whole = whole + qr[k, g, 0:heads]
-                square = square + qr[k, g, heads:QROWS]
-            inverse = lax.rsqrt(square / total + norm_eps)
-            query = rounded(rotate(whole * inverse, g))
-            score = lax.dot_general(query.astype(bf16), kb[g], (((1,), (1,)), ((), ())), preferred_element_type=f32)
-            new_key = rounded(rotate(jnp.broadcast_to(fresh_sum[2 * g:2 * g + 1] * inverse, (heads, hd)), g))
-            new_value = rounded(fresh_sum[2 * g + 1:2 * g + 2] * inverse)
-            own = jnp.sum(query * new_key, axis=1, keepdims=True) * scale + own_mask
-            masked = score * scale + bias[g]
-            top = jnp.maximum(jnp.max(masked, axis=1, keepdims=True), own)
-            weight = jnp.exp(masked - top)
-            fresh = jnp.exp(own - top)
-            denominator = jnp.sum(weight, axis=1, keepdims=True) + fresh
-            numerator = jnp.dot(weight.astype(bf16), vb[g], preferred_element_type=f32) + rounded(fresh) * new_value
-            orr[me, g * heads:(g + 1) * heads, :] = numerator / denominator
-            stats.append(top + jnp.log(denominator))
-        orr[me, 2 * heads:3 * heads, :] = jnp.where(low, stats[0], stats[1])
-        oc = []
-        for k, (p, _, _) in enumerate(peers):
-            c = pltpu.make_async_remote_copy(
-                src_ref=orr.at[me], dst_ref=orr.at[me], send_sem=os_sem.at[k], recv_sem=or_sem.at[k],
-                device_id={"ctx": p}, device_id_type=MESH)
-            c.start()
-            oc.append(c)
+
+        @pl.when(core == 0)
+        def _():
+            for c in q_copies(n - 1):
+                c.start()
+            taken(kst.at[l], hs_sem.at[l, 0])
+            taken(vst.at[l], hs_sem.at[l, 1])
+
+        @pl.when(core == 1)
+        def _():
+            blocks = 2 * side
+            taken(kst.at[l, pl.ds(0, blocks - 2)], hs_sem.at[l, 0])
+            taken(vst.at[l, pl.ds(0, blocks - 2)], hs_sem.at[l, 1])
+            for h in (1, 0):
+                taken(krv.at[l, h, pl.ds(0, blocks - 2 * h)], hr_sem.at[l, h, 0])
+                taken(vrv.at[l, h, pl.ds(0, blocks - 2 * h)], hr_sem.at[l, h, 1])
+                for g in range(2):
+                    part = slice(g * side, (g + 1) * side)
+                    kb[h, g] = krv[l, h, part].reshape(side * span, hd).astype(bf16)
+                    vb[h, g] = vrv[l, h, part].reshape(side * span, hd).astype(bf16)
+
+            @pl.when(y == x)
+            def _():
+                kr[1, me] = ks[pl.ds(pl.multiple_of(8 * x, 8), 4), :]
+                for h in (1, 0):
+                    taken(kr.at[h, pl.ds(0, n - h)], kr_sem.at[h])
+                    fresh_sum[h] = functools.reduce(jnp.add, [kr[h, c] for c in range(n)])
+
+            for h in (1, 0):
+                q_arrivals(h)
+                attend(h)
+                for k in range(n - h):
+                    o_copy(h, k).start()
 
         @pl.when(l + 1 < layers)
         def _():
             stage(l + 1)
 
         load(WO, l).wait()
-        for c in qc:
-            c.wait_send()
-        for d in range(side):
-            @pl.when(me != d * side + d)
-            def _():
-                fresh_copy(d).wait_send()
-        for c in oc:
-            c.wait_recv()
+        for k in far_chips:
+            for c in q_copies(k):
+                c.wait_send()
+        fresh_sends(lambda c: c.wait_send())
+
+        @pl.when(core == 0)
+        def _():
+            for c in q_copies(n - 1):
+                c.wait_send()
+            taken(orr.at[me], or_sem.at[n - 1])
+
+        for k in far_chips:
+            taken(orr.at[places[k][0]], or_sem.at[k])
 
         @pl.when(l + 1 < layers)
         def _():
-            for c in ship(l + 1):
-                c.start()
+            ship_start(l + 1)
 
         logs = [orr[c, 2 * heads:3 * heads, :] for c in range(n)]
         groups = [[[r * side + b for r in range(side)] for b in range(side)],
@@ -270,8 +331,12 @@
                     recv_sem=tr_sem.at[odd, i, k], device_id={"tp": p}, device_id_type=MESH)
                 c.start()
                 ts.append(c)
-        for c in oc:
-            c.wait_send()
+        @pl.when(core == 1)
+        def _():
+            for h in (1, 0):
+                for k in range(n - h):
+                    o_copy(h, k).wait_send()
+
         for i in range(pieces):
             cut = slice(i * piece, (i + 1) * piece)
             moved = out_ref[:, cut] + tps[i]
@@ -316,26 +381,27 @@
             pltpu.VMEM((2, heads, hd), f32),
             pltpu.VMEM((2, heads, hd), f32),
             pltpu.VMEM((batch * 16, hd), f32),
-            pltpu.VMEM((n - 1, 2, 16, hd), f32),
+            pltpu.VMEM((2, n, 2, 16, hd), f32),
             pltpu.VMEM((side * 8, hd), f32),
-            pltpu.VMEM((n, 4, hd), f32),
-            pltpu.VMEM((4, hd), f32),
+            pltpu.VMEM((2, n, 4, hd), f32),
+            pltpu.VMEM((2, 4, hd), f32),
             pltpu.VMEM((layers, batch, span, hd), f32),
             pltpu.VMEM((layers, batch, span, hd), f32),
-            pltpu.VMEM((layers, 2, side, span, hd), f32),
-            pltpu.VMEM((layers, 2, side, span, hd), f32),
-            pltpu.VMEM((2, side * span, hd), bf16),
-            pltpu.VMEM((2, side * span, hd), bf16),
+            pltpu.VMEM((layers, 2, 2 * side, span, hd), f32),
+            pltpu.VMEM((layers, 2, 2 * side, span, hd), f32),
+            pltpu.VMEM((2, 2, side * span, hd), bf16),
+            pltpu.VMEM((2, 2, side * span, hd), bf16),
             pltpu.VMEM((n, 3 * heads, hd), f32),
+            pltpu.VMEM((3 * heads, hd), f32),
             pltpu.VMEM((batch * heads, hd), f32),
             pltpu.VMEM((pieces, batch, feat // pieces), f32),
             pltpu.VMEM((2, pieces, tn - 1, batch, feat // pieces), f32),
             dma((6, layers)),
-            dma((n - 1, 2)), dma((n - 1, 2)),
-            dma((side,)), dma(()),
-            dma((n - 1,)), dma((n - 1,)),
+            dma((n, 2)), dma((2, n, 2)),
+            dma((side,)), dma((2,)),
+            dma((2, n)), dma((n,)),
             dma((pieces, tn - 1)), dma((2, pieces, tn - 1)),
-            dma((layers, 2, 2, side - 1)), dma((layers, 2, 2, side - 1)),
+            dma((layers, 2)), dma((layers, 2, 2)),
             dma((3,)), pltpu.SemaphoreType.REGULAR,
         ],
         compiler_params=pltpu.CompilerParams(

time: 75.9 us -> 74.4 us (0.980)
  Pallas kernels: 75.2 us -> 73.6 us
    pallas_call x1, Pallas kernels: 75.2 us -> 73.6 us  [shards(): pl.pallas_call(functools.partial(kernel, dims), out_shape=pltpu.VMEM((bat...]
where the time goes in v5:
time: 74.4 us; the launch traced here: 74.3 us
  Pallas kernels  73.6 us (99%)
    pallas_call x1, Pallas kernels, shards(): pl.pallas_call(functools.partial(kernel, dims), out_shape=pltpu.VMEM((bat...  73.6 us

profile of v5, /device:TPU:1, one launch (start us, length us, event | category | flops | bytes accessed | tf_op | source)
XLA Modules:
  0.0 74.3 jit_solution(4218197658458008760)
XLA Ops:
  0.0 73.6 %shard_map.91 = f32[8,512]{1,0:T(8,128)S(1)} custom-call(bf16[8,512]{1,0:T(8,128)(2,1)} %hidden_h.1, bf16[4,512]{1,0:T(4,128)(2,1)} %gains_h.1, s32[8]{0:T(128)} %lengths_h.1, bf16[4,512,1024]{2,1,0:T(8,128)(2,1)} %wq_h.1, bf16[4,512,128]{2,1,0:T(8,128)(2,1)} %wk_h.1, bf16[4,512,128]{2,1,0:T(8,128)(2,1)} %wv_h.1, bf16[4,1024,512]{2,1,0:T(8,128)(2,1)} %wo_h.1, ...), custom_call_target="tpu_custom_call" | custom-call | tf_op jit(solution)/shard_map/pallas_call | solution.py:371
  73.7 0.6 copy.11

commit v6 on v5

--- a/solution.py
+++ b/solution.py
@@ -175,8 +175,9 @@
         return u.astype(bf16).astype(f32)
 
     def attend(h):
-        stats = []
-        for g in range(2):
+        both = range(2)
+        inverse, query = [], []
+        for g in both:
             whole, square = qr[h, 0, g, 0:heads], qr[h, 0, g, heads:QROWS]
             for k in range(1, n - h):
                 whole = whole + qr[h, k, g, 0:heads]
@@ -185,29 +186,28 @@
                 at = pl.multiple_of(mine[g] * 16, 16)
                 whole = whole + qs[pl.ds(at, heads), :]
                 square = square + qs[pl.ds(pl.multiple_of(at + 8, 8), 1), :]
-            inverse = lax.rsqrt(square / total + norm_eps)
-            query = rounded(rotate(whole * inverse, g))
-            score = lax.dot_general(
-                query.astype(bf16), kb[h, g], (((1,), (1,)), ((), ())), preferred_element_type=f32)
-            new_key = fresh_sum[h, 2 * g:2 * g + 1] * inverse
-            new_key = rounded(rotate(jnp.broadcast_to(new_key, (heads, hd)), g))
-            new_value = rounded(fresh_sum[h, 2 * g + 1:2 * g + 2] * inverse)
-            own = jnp.sum(query * new_key, axis=1, keepdims=True) * scale + own_mask
-            masked = score * scale + bias[g]
-            top = jnp.maximum(jnp.max(masked, axis=1, keepdims=True), own)
-            weight = jnp.exp(masked - top)
-            fresh = jnp.exp(own - top)
-            denominator = jnp.sum(weight, axis=1, keepdims=True) + fresh
-            numerator = jnp.dot(weight.astype(bf16), vb[h, g], preferred_element_type=f32) + rounded(fresh) * new_value
+            inverse.append(lax.rsqrt(square / total + norm_eps))
+            query.append(rounded(rotate(whole * inverse[g], g)))
+        score = [lax.dot_general(
+            query[g].astype(bf16), kb[h, g], (((1,), (1,)), ((), ())), preferred_element_type=f32) for g in both]
+        new_key = [rounded(rotate(jnp.broadcast_to(fresh_sum[h, 2 * g:2 * g + 1] * inverse[g], (heads, hd)), g)) for g in both]
+        new_value = [rounded(fresh_sum[h, 2 * g + 1:2 * g + 2] * inverse[g]) for g in both]
+        own = [jnp.sum(query[g] * new_key[g], axis=1, keepdims=True) * scale + own_mask for g in both]
+        masked = [score[g] * scale + bias[g] for g in both]
+        top = [jnp.maximum(jnp.max(masked[g], axis=1, keepdims=True), own[g]) for g in both]
+        weight = [jnp.exp(masked[g] - top[g]) for g in both]
+        numerator = [jnp.dot(weight[g].astype(bf16), vb[h, g], preferred_element_type=f32) for g in both]
+        fresh = [jnp.exp(own[g] - top[g]) for g in both]
+        denominator = [jnp.sum(weight[g], axis=1, keepdims=True) + fresh[g] for g in both]
+        logs = [top[g] + jnp.log(denominator[g]) for g in both]
+        share = [1.0 / denominator[g] for g in both]
+        parts = [(numerator[g] + rounded(fresh[g]) * new_value[g]) * share[g] for g in both]
+        parts.append(jnp.where(low, logs[0], logs[1]))
+        for i, part in enumerate(parts):
             if h:
-                orr[me, g * heads:(g + 1) * heads, :] = numerator / denominator
+                orr[me, i * heads:(i + 1) * heads, :] = part
             else:
-                od[g * heads:(g + 1) * heads, :] = numerator / denominator
-            stats.append(top + jnp.log(denominator))
-        if h:
-            orr[me, 2 * heads:3 * heads, :] = jnp.where(low, stats[0], stats[1])
-        else:
-            od[2 * heads:3 * heads, :] = jnp.where(low, stats[0], stats[1])
+                od[i * heads:(i + 1) * heads, :] = part
 
     def layer_step(l, carry):
         stream = out_ref[...]
@@ -229,11 +229,11 @@
             kv = jnp.dot(scaled, w[l], preferred_element_type=f32)
             for g in range(2):
                 ks[pl.ds(2 * g + i, side, stride=8), :] = kv[g * side:(g + 1) * side]
-        fresh_sends(lambda c: c.start())
         put(heads, jnp.broadcast_to(squares, (batch, hd)))
         q = jnp.dot(scaled, wq[l], preferred_element_type=f32)
         for h in range(heads):
             put(h, q[:, h * hd:(h + 1) * hd])
+        fresh_sends(lambda c: c.start())
         for k in far_chips:
             for c in q_copies(k):
                 c.start()

time: 74.4 us -> 73.7 us (level)
  no operation moved by 1% of the time
where the time goes in v6:
time: 73.7 us; the launch traced here: 73.5 us
  Pallas kernels  72.9 us (99%)
    pallas_call x1, Pallas kernels, shards(): pl.pallas_call(functools.partial(kernel, dims), out_shape=pltpu.VMEM((bat...  72.9 us

profile of v6, /device:TPU:1, one launch (start us, length us, event | category | flops | bytes accessed | tf_op | source)
XLA Modules:
  0.0 73.5 jit_solution(12780588780976207851)
XLA Ops:
  0.0 72.9 %shard_map.91 = f32[8,512]{1,0:T(8,128)S(1)} custom-call(bf16[8,512]{1,0:T(8,128)(2,1)} %hidden_h.1, bf16[4,512]{1,0:T(4,128)(2,1)} %gains_h.1, s32[8]{0:T(128)} %lengths_h.1, bf16[4,512,1024]{2,1,0:T(8,128)(2,1)} %wq_h.1, bf16[4,512,128]{2,1,0:T(8,128)(2,1)} %wk_h.1, bf16[4,512,128]{2,1,0:T(8,128)(2,1)} %wv_h.1, bf16[4,1024,512]{2,1,0:T(8,128)(2,1)} %wo_h.1, ...), custom_call_target="tpu_custom_call" | custom-call | tf_op jit(solution)/shard_map/pallas_call | solution.py:371
  72.9 0.6 copy.11

commit v7 on v6

--- a/solution.py
+++ b/solution.py
@@ -17,11 +17,9 @@
 
 def kernel(dims, hidden_h, gains_h, lengths_h, wq_h, wk_h, wv_h, wo_h, kc_h, vc_h, out_ref,
            hidden_ref, gains_ref, lengths_ref, wq, wk, wv, wo, kc, vc, gain, bias, cosine, sine, qs, qr, ks, kr, fresh_sum, kst, vst, krv, vrv, kb, vb,
-           orr, od, cm, tps, tpr, w_sem, qs_sem, qr_sem, ks_sem, kr_sem, os_sem, or_sem, ts_sem, tr_sem, hs_sem, hr_sem, small_sem, ready):
+           orr, cm, wst, wo2, wob, tps, tpr, w_sem, qs_sem, qr_sem, ks_sem, kr_sem, os_sem, or_sem, ts_sem, tr_sem, hs_sem, hr_sem, xs_sem, xr_sem, small_sem, ready, go):
     n, tn, side, layers, batch, feat, total, heads, hd, span = dims
     f32, bf16 = jnp.float32, jnp.bfloat16
-    pieces = tps.shape[0]
-    piece = feat // pieces
     scale = 1.0 / math.sqrt(hd)
     me = lax.axis_index("ctx")
     mt = lax.axis_index("tp")
@@ -156,8 +154,31 @@
 
     def o_copy(h, k):
         return pltpu.make_async_remote_copy(
-            src_ref=orr.at[me] if h else od, dst_ref=orr.at[me], send_sem=os_sem.at[h, k], recv_sem=or_sem.at[k],
-            device_id={"ctx": places[k][0], "tp": cores[h]}, device_id_type=MESH)
+            src_ref=orr.at[h, me], dst_ref=orr.at[h, me], send_sem=os_sem.at[h, k], recv_sem=or_sem.at[h, k],
+            device_id={"ctx": places[k][0]}, device_id_type=MESH)
+
+    def w_out_copy(l):
+        return pltpu.make_async_remote_copy(
+            src_ref=wst.at[l], dst_ref=wo2.at[l], send_sem=xs_sem.at[l], recv_sem=xr_sem.at[l],
+            device_id={"tp": cores[1]}, device_id_type=MESH)
+
+    def w_out_start(l):
+        load(WO, l).wait()
+        wst[l] = wo[l].astype(f32)
+        w_out_copy(l).start()
+
+    def t_copy(odd, k):
+        return pltpu.make_async_remote_copy(
+            src_ref=tps, dst_ref=tpr.at[odd, k], send_sem=ts_sem.at[k], recv_sem=tr_sem.at[odd, k],
+            device_id={"tp": tpeers[k]}, device_id_type=MESH)
+
+    def t_arrivals(odd, cross):
+        moved = None
+        for k, (dz, dc) in enumerate(toffsets):
+            if dc == cross:
+                taken(tpr.at[odd, k], tr_sem.at[odd, k])
+                moved = tpr[odd, k] if moved is None else moved + tpr[odd, k]
+        return moved
 
     fresh_sum[...] = jnp.zeros_like(fresh_sum)
     stage(0)
@@ -204,10 +225,35 @@
         parts = [(numerator[g] + rounded(fresh[g]) * new_value[g]) * share[g] for g in both]
         parts.append(jnp.where(low, logs[0], logs[1]))
         for i, part in enumerate(parts):
-            if h:
-                orr[me, i * heads:(i + 1) * heads, :] = part
-            else:
-                od[i * heads:(i + 1) * heads, :] = part
+            orr[h, me, i * heads:(i + 1) * heads, :] = part
+
+    def merge(h):
+        logs = [orr[h, c, 2 * heads:3 * heads, :] for c in range(n)]
+        groups = [[[r * side + b for r in range(side)] for b in range(side)],
+                  [[b * side + r for r in range(side)] for b in range(side)]]
+
+        def over(values, op):
+            return [[functools.reduce(op, [values[c] for c in group]) for group in part] for part in groups]
+
+        def split(pair, c):
+            return jnp.where(low, pair[0][c % side], pair[1][c // side])
+
+        largest = over(logs, jnp.maximum)
+        factors = [jnp.exp(logs[c] - split(largest, c)) for c in range(n)]
+        sums = over(factors, jnp.add)
+        inverses = [[1.0 / s for s in part] for part in sums]
+        factors = [factors[c] * split(inverses, c) for c in range(n)]
+        swapped = [pltpu.roll(f, half, 1) for f in factors]
+        for g in range(2):
+            for b, group in enumerate(groups[g]):
+                merged = None
+                for c in group:
+                    factor = jnp.where(low, factors[c], swapped[c]) if g == 0 else jnp.where(low, swapped[c], factors[c])
+                    term = orr[h, c, g * heads:(g + 1) * heads, :] * factor
+                    merged = term if merged is None else merged + term
+                at = (g * side + b) * heads
+                cm[h, at:at + heads, :] = merged
+        return jnp.concatenate([cm[h, pl.ds(t, batch, stride=heads), :] for t in range(heads)], axis=1).astype(bf16)
 
     def layer_step(l, carry):
         stream = out_ref[...]
@@ -238,12 +284,44 @@
             for c in q_copies(k):
                 c.start()
 
+        odd = lax.rem(l, 2)
+        more = l + 1 < layers
+
         @pl.when(core == 0)
         def _():
             for c in q_copies(n - 1):
                 c.start()
+
+            @pl.when(l == 0)
+            def _():
+                w_out_start(0)
+
+            @pl.when(more)
+            def _():
+                stage(l + 1)
+                w_out_start(l + 1)
+
             taken(kst.at[l], hs_sem.at[l, 0])
             taken(vst.at[l], hs_sem.at[l, 1])
+            for k in range(n):
+                for c in q_copies(k):
+                    c.wait_send()
+            fresh_sends(lambda c: c.wait_send())
+
+            @pl.when(more)
+            def _():
+                pl.semaphore_wait(go, 1)
+                ship_start(l + 1)
+
+            out_ref[...] = out_ref[...] + t_arrivals(odd, 1)
+
+            @pl.when(l == 0)
+            def _():
+                w_out_copy(0).wait_send()
+
+            @pl.when(more)
+            def _():
+                w_out_copy(l + 1).wait_send()
 
         @pl.when(core == 1)
         def _():
@@ -268,84 +346,46 @@
             for h in (1, 0):
                 q_arrivals(h)
                 attend(h)
-                for k in range(n - h):
+                for k in far_chips:
                     o_copy(h, k).start()
 
-        @pl.when(l + 1 < layers)
-        def _():
-            stage(l + 1)
-
-        load(WO, l).wait()
-        for k in far_chips:
-            for c in q_copies(k):
-                c.wait_send()
-        fresh_sends(lambda c: c.wait_send())
-
-        @pl.when(core == 0)
-        def _():
-            for c in q_copies(n - 1):
-                c.wait_send()
-            taken(orr.at[me], or_sem.at[n - 1])
-
-        for k in far_chips:
-            taken(orr.at[places[k][0]], or_sem.at[k])
-
-        @pl.when(l + 1 < layers)
-        def _():
-            ship_start(l + 1)
-
-        logs = [orr[c, 2 * heads:3 * heads, :] for c in range(n)]
-        groups = [[[r * side + b for r in range(side)] for b in range(side)],
-                  [[b * side + r for r in range(side)] for b in range(side)]]
-
-        def over(values, op):
-            return [[functools.reduce(op, [values[c] for c in group]) for group in part] for part in groups]
-
-        def split(pair, c):
-            return jnp.where(low, pair[0][c % side], pair[1][c // side])
-
-        largest = over(logs, jnp.maximum)
-        factors = [jnp.exp(logs[c] - split(largest, c)) for c in range(n)]
-        sums = over(factors, jnp.add)
-        inverses = [[1.0 / s for s in part] for part in sums]
-        factors = [factors[c] * split(inverses, c) for c in range(n)]
-        swapped = [pltpu.roll(f, half, 1) for f in factors]
-        for g in range(2):
-            for b, group in enumerate(groups[g]):
-                merged = None
-                for c in group:
-                    factor = jnp.where(low, factors[c], swapped[c]) if g == 0 else jnp.where(low, swapped[c], factors[c])
-                    term = orr[c, g * heads:(g + 1) * heads, :] * factor
-                    merged = term if merged is None else merged + term
-                at = (g * side + b) * heads
-                cm[at:at + heads, :] = merged
-        context = jnp.concatenate([cm[pl.ds(h, batch, stride=heads), :] for h in range(heads)], axis=1).astype(bf16)
-        odd = lax.rem(l, 2)
-        ts = []
-        for i in range(pieces):
-            cut = slice(i * piece, (i + 1) * piece)
-            tps[i] = jnp.dot(context, wo[l, :, cut], preferred_element_type=f32)
-            for k, p in enumerate(tpeers):
-                c = pltpu.make_async_remote_copy(
-                    src_ref=tps.at[i], dst_ref=tpr.at[odd, i, k], send_sem=ts_sem.at[i, k],
-                    recv_sem=tr_sem.at[odd, i, k], device_id={"tp": p}, device_id_type=MESH)
-                c.start()
-                ts.append(c)
-        @pl.when(core == 1)
-        def _():
+            @pl.when(more)
+            def _():
+                stage(l + 1)
+
+            load(WO, l).wait()
+            taken(wo2.at[l], xr_sem.at[l])
+            wob[...] = wo2[l].astype(bf16)
+            for k in far_chips:
+                for c in q_copies(k):
+                    c.wait_send()
+            fresh_sends(lambda c: c.wait_send())
+            for k in far_chips[11:]:
+                taken(orr.at[1, places[k][0]], or_sem.at[1, k])
+            @pl.when(more)
+            def _():
+                pl.semaphore_signal(go, inc=1, device_id={"tp": cores[0]}, device_id_type=MESH)
+
+            @pl.when(more)
+            def _():
+                ship_start(l + 1)
+
+            for k in far_chips[:11]:
+                taken(orr.at[1, places[k][0]], or_sem.at[1, k])
+            tps[...] = jnp.dot(merge(1), wo[l], preferred_element_type=f32)
+            for k in far_chips:
+                taken(orr.at[0, places[k][0]], or_sem.at[0, k])
+
+            tps[...] = tps[...] + jnp.dot(merge(0), wob[...], preferred_element_type=f32)
+            for k in range(tn - 1):
+                t_copy(odd, k).start()
             for h in (1, 0):
-                for k in range(n - h):
+                for k in far_chips:
                     o_copy(h, k).wait_send()
-
-        for i in range(pieces):
-            cut = slice(i * piece, (i + 1) * piece)
-            moved = out_ref[:, cut] + tps[i]
+            out_ref[...] = out_ref[...] + tps[...] + t_arrivals(odd, 0)
             for k in range(tn - 1):
-                ts[i * (tn - 1) + k].wait_recv()
-                moved = moved + tpr[odd, i, k]
-            out_ref[:, cut] = moved
-        for c in ts:
-            c.wait_send()
+                t_copy(odd, k).wait_send()
+
         return carry
 
     lax.fori_loop(0, layers, layer_step, 0)
@@ -359,7 +399,6 @@
     heads = columns // hd
     side = math.isqrt(n)
     dims = (n, tn, side, layers, batch, feat, feat * n, heads, hd, span)
-    pieces = 1
     f32, bf16 = jnp.float32, jnp.bfloat16
     vmem = pl.BlockSpec(memory_space=pltpu.VMEM)
     far = pl.BlockSpec(memory_space=pl.ANY)
@@ -391,18 +430,21 @@
             pltpu.VMEM((layers, 2, 2 * side, span, hd), f32),
             pltpu.VMEM((2, 2, side * span, hd), bf16),
             pltpu.VMEM((2, 2, side * span, hd), bf16),
-            pltpu.VMEM((n, 3 * heads, hd), f32),
-            pltpu.VMEM((3 * heads, hd), f32),
-            pltpu.VMEM((batch * heads, hd), f32),
-            pltpu.VMEM((pieces, batch, feat // pieces), f32),
-            pltpu.VMEM((2, pieces, tn - 1, batch, feat // pieces), f32),
+            pltpu.VMEM((2, n, 3 * heads, hd), f32),
+            pltpu.VMEM((2, batch * heads, hd), f32),
+            pltpu.VMEM(w_out.shape, f32),
+            pltpu.VMEM(w_out.shape, f32),
+            pltpu.VMEM(w_out.shape[1:], bf16),
+            pltpu.VMEM((batch, feat), f32),
+            pltpu.VMEM((2, tn - 1, batch, feat), f32),
             dma((6, layers)),
             dma((n, 2)), dma((2, n, 2)),
             dma((side,)), dma((2,)),
-            dma((2, n)), dma((n,)),
-            dma((pieces, tn - 1)), dma((2, pieces, tn - 1)),
+            dma((2, n)), dma((2, n)),
+            dma((tn - 1,)), dma((2, tn - 1)),
             dma((layers, 2)), dma((layers, 2, 2)),
-            dma((3,)), pltpu.SemaphoreType.REGULAR,
+            dma((layers,)), dma((layers,)),
+            dma((3,)), pltpu.SemaphoreType.REGULAR, pltpu.SemaphoreType.REGULAR,
         ],
         compiler_params=pltpu.CompilerParams(
             collective_id=0, has_side_effects=True, vmem_limit_bytes=60 * 1024 * 1024),

time: 73.7 us -> 70.6 us (0.958)
  Pallas kernels: 72.9 us -> 69.7 us
    pallas_call x1, Pallas kernels: 72.9 us -> 69.7 us  [shards(): pl.pallas_call(functools.partial(kernel, dims), out_shape=pltpu.VMEM((bat...]
where the time goes in v7:
time: 70.6 us; the launch traced here: 70.3 us
  Pallas kernels  69.7 us (99%)
    pallas_call x1, Pallas kernels, shards(): pl.pallas_call(functools.partial(kernel, dims), out_shape=pltpu.VMEM((bat...  69.7 us

profile of v7, /device:TPU:1, one launch (start us, length us, event | category | flops | bytes accessed | tf_op | source)
XLA Modules:
  0.0 70.3 jit_solution(7400481459026799787)
XLA Ops:
  0.0 69.7 %shard_map.91 = f32[8,512]{1,0:T(8,128)S(1)} custom-call(bf16[8,512]{1,0:T(8,128)(2,1)} %hidden_h.1, bf16[4,512]{1,0:T(4,128)(2,1)} %gains_h.1, s32[8]{0:T(128)} %lengths_h.1, bf16[4,512,1024]{2,1,0:T(8,128)(2,1)} %wq_h.1, bf16[4,512,128]{2,1,0:T(8,128)(2,1)} %wk_h.1, bf16[4,512,128]{2,1,0:T(8,128)(2,1)} %wv_h.1, bf16[4,1024,512]{2,1,0:T(8,128)(2,1)} %wo_h.1, ...), custom_call_target="tpu_custom_call" | custom-call | tf_op jit(solution)/shard_map/pallas_call | solution.py:410
  69.7 0.6 copy.11

commit v8 on v7

--- a/solution.py
+++ b/solution.py
@@ -13,6 +13,7 @@
 rope_base = 500000.0
 MESH = pl.DeviceIdType.MESH
 QROWS = 9
+ROWS = 17
 
 
 def kernel(dims, hidden_h, gains_h, lengths_h, wq_h, wk_h, wv_h, wo_h, kc_h, vc_h, out_ref,
@@ -70,6 +71,8 @@
     half = hd // 2
     lane = lax.broadcasted_iota(jnp.int32, (heads, hd), 1)
     low = lane < half
+    head = lax.broadcasted_iota(jnp.int32, (heads, hd), 0)
+    picks = (lane == head, lane == head + half)
     mine = (x, side + y)
     slot = lax.broadcasted_iota(jnp.int32, (heads, side * span), 1)
     block = slot // span
@@ -154,7 +157,7 @@
 
     def o_copy(h, k):
         return pltpu.make_async_remote_copy(
-            src_ref=orr.at[h, me], dst_ref=orr.at[h, me], send_sem=os_sem.at[h, k], recv_sem=or_sem.at[h, k],
+            src_ref=orr.at[h, me, pl.ds(0, ROWS)], dst_ref=orr.at[h, me, pl.ds(0, ROWS)], send_sem=os_sem.at[h, k], recv_sem=or_sem.at[h, k],
             device_id={"ctx": places[k][0]}, device_id_type=MESH)
 
     def w_out_copy(l):
@@ -223,12 +226,13 @@
         logs = [top[g] + jnp.log(denominator[g]) for g in both]
         share = [1.0 / denominator[g] for g in both]
         parts = [(numerator[g] + rounded(fresh[g]) * new_value[g]) * share[g] for g in both]
-        parts.append(jnp.where(low, logs[0], logs[1]))
-        for i, part in enumerate(parts):
-            orr[h, me, i * heads:(i + 1) * heads, :] = part
+        for g in both:
+            orr[h, me, g * heads:(g + 1) * heads, :] = parts[g]
+        spread = jnp.where(picks[0], logs[0], jnp.where(picks[1], logs[1], 0.0))
+        orr[h, me, 2 * heads:ROWS, :] = jnp.sum(spread, axis=0, keepdims=True)
 
     def merge(h):
-        logs = [orr[h, c, 2 * heads:3 * heads, :] for c in range(n)]
+        logs = [orr[h, c, 2 * heads:ROWS, :] for c in range(n)]
         groups = [[[r * side + b for r in range(side)] for b in range(side)],
                   [[b * side + r for r in range(side)] for b in range(side)]]
 
@@ -236,19 +240,19 @@
             return [[functools.reduce(op, [values[c] for c in group]) for group in part] for part in groups]
 
         def split(pair, c):
-            return jnp.where(low, pair[0][c % side], pair[1][c // side])
+            return jnp.where(low[0:1], pair[0][c % side], pair[1][c // side])
 
         largest = over(logs, jnp.maximum)
         factors = [jnp.exp(logs[c] - split(largest, c)) for c in range(n)]
         sums = over(factors, jnp.add)
         inverses = [[1.0 / s for s in part] for part in sums]
         factors = [factors[c] * split(inverses, c) for c in range(n)]
-        swapped = [pltpu.roll(f, half, 1) for f in factors]
+        factors = [jnp.broadcast_to(f, (heads, hd)) for f in factors]
         for g in range(2):
             for b, group in enumerate(groups[g]):
                 merged = None
                 for c in group:
-                    factor = jnp.where(low, factors[c], swapped[c]) if g == 0 else jnp.where(low, swapped[c], factors[c])
+                    factor = jnp.sum(jnp.where(picks[g], factors[c], 0.0), axis=1, keepdims=True)
                     term = orr[h, c, g * heads:(g + 1) * heads, :] * factor
                     merged = term if merged is None else merged + term
                 at = (g * side + b) * heads
@@ -336,14 +340,14 @@
                     kb[h, g] = krv[l, h, part].reshape(side * span, hd).astype(bf16)
                     vb[h, g] = vrv[l, h, part].reshape(side * span, hd).astype(bf16)
 
-            @pl.when(y == x)
-            def _():
-                kr[1, me] = ks[pl.ds(pl.multiple_of(8 * x, 8), 4), :]
-                for h in (1, 0):
+            for h in (1, 0):
+                @pl.when(y == x)
+                def _():
+                    if h:
+                        kr[1, me] = ks[pl.ds(pl.multiple_of(8 * x, 8), 4), :]
                     taken(kr.at[h, pl.ds(0, n - h)], kr_sem.at[h])
                     fresh_sum[h] = functools.reduce(jnp.add, [kr[h, c] for c in range(n)])
 
-            for h in (1, 0):
                 q_arrivals(h)
                 attend(h)
                 for k in far_chips:
@@ -360,8 +364,8 @@
                 for c in q_copies(k):
                     c.wait_send()
             fresh_sends(lambda c: c.wait_send())
-            for k in far_chips[11:]:
-                taken(orr.at[1, places[k][0]], or_sem.at[1, k])
+            for k in far_chips[13:15]:
+                taken(orr.at[1, places[k][0], pl.ds(0, ROWS)], or_sem.at[1, k])
             @pl.when(more)
             def _():
                 pl.semaphore_signal(go, inc=1, device_id={"tp": cores[0]}, device_id_type=MESH)
@@ -370,11 +374,11 @@
             def _():
                 ship_start(l + 1)
 
-            for k in far_chips[:11]:
-                taken(orr.at[1, places[k][0]], or_sem.at[1, k])
+            for k in far_chips[0:13]:
+                taken(orr.at[1, places[k][0], pl.ds(0, ROWS)], or_sem.at[1, k])
             tps[...] = jnp.dot(merge(1), wo[l], preferred_element_type=f32)
             for k in far_chips:
-                taken(orr.at[0, places[k][0]], or_sem.at[0, k])
+                taken(orr.at[0, places[k][0], pl.ds(0, ROWS)], or_sem.at[0, k])
 
             tps[...] = tps[...] + jnp.dot(merge(0), wob[...], preferred_element_type=f32)
             for k in range(tn - 1):

time: 70.6 us -> 68.4 us (0.969)
  Pallas kernels: 69.7 us -> 67.5 us
    pallas_call x1, Pallas kernels: 69.7 us -> 67.5 us  [shards(): pl.pallas_call(functools.partial(kernel, dims), out_shape=pltpu.VMEM((bat...]
where the time goes in v8:
time: 68.4 us; the launch traced here: 68.1 us
  Pallas kernels  67.5 us (99%)
    pallas_call x1, Pallas kernels, shards(): pl.pallas_call(functools.partial(kernel, dims), out_shape=pltpu.VMEM((bat...  67.5 us

profile of v8, /device:TPU:1, one launch (start us, length us, event | category | flops | bytes accessed | tf_op | source)
XLA Modules:
  0.0 68.1 jit_solution(16205342780437515434)
XLA Ops:
  0.0 67.5 %shard_map.91 = f32[8,512]{1,0:T(8,128)S(1)} custom-call(bf16[8,512]{1,0:T(8,128)(2,1)} %hidden_h.1, bf16[4,512]{1,0:T(4,128)(2,1)} %gains_h.1, s32[8]{0:T(128)} %lengths_h.1, bf16[4,512,1024]{2,1,0:T(8,128)(2,1)} %wq_h.1, bf16[4,512,128]{2,1,0:T(8,128)(2,1)} %wk_h.1, bf16[4,512,128]{2,1,0:T(8,128)(2,1)} %wv_h.1, bf16[4,1024,512]{2,1,0:T(8,128)(2,1)} %wo_h.1, ...), custom_call_target="tpu_custom_call" | custom-call | tf_op jit(solution)/shard_map/pallas_call | solution.py:414
  67.5 0.6 copy.11

commit v9 on v8

--- a/solution.py
+++ b/solution.py
@@ -364,7 +364,7 @@
                 for c in q_copies(k):
                     c.wait_send()
             fresh_sends(lambda c: c.wait_send())
-            for k in far_chips[13:15]:
+            for k in far_chips[14:15]:
                 taken(orr.at[1, places[k][0], pl.ds(0, ROWS)], or_sem.at[1, k])
             @pl.when(more)
             def _():
@@ -374,7 +374,7 @@
             def _():
                 ship_start(l + 1)
 
-            for k in far_chips[0:13]:
+            for k in far_chips[0:14]:
                 taken(orr.at[1, places[k][0], pl.ds(0, ROWS)], or_sem.at[1, k])
             tps[...] = jnp.dot(merge(1), wo[l], preferred_element_type=f32)
             for k in far_chips:

time: 68.4 us -> 67.7 us (0.990)
  no operation moved by 1% of the time
where the time goes in v9:
time: 67.7 us; the launch traced here: 67.5 us
  Pallas kernels  66.9 us (99%)
    pallas_call x1, Pallas kernels, shards(): pl.pallas_call(functools.partial(kernel, dims), out_shape=pltpu.VMEM((bat...  66.9 us

profile of v9, /device:TPU:1, one launch (start us, length us, event | category | flops | bytes accessed | tf_op | source)
XLA Modules:
  0.0 67.5 jit_solution(8349680876400361730)
XLA Ops:
  0.0 66.9 %shard_map.91 = f32[8,512]{1,0:T(8,128)S(1)} custom-call(bf16[8,512]{1,0:T(8,128)(2,1)} %hidden_h.1, bf16[4,512]{1,0:T(4,128)(2,1)} %gains_h.1, s32[8]{0:T(128)} %lengths_h.1, bf16[4,512,1024]{2,1,0:T(8,128)(2,1)} %wq_h.1, bf16[4,512,128]{2,1,0:T(8,128)(2,1)} %wk_h.1, bf16[4,512,128]{2,1,0:T(8,128)(2,1)} %wv_h.1, bf16[4,1024,512]{2,1,0:T(8,128)(2,1)} %wo_h.1, ...), custom_call_target="tpu_custom_call" | custom-call | tf_op jit(solution)/shard_map/pallas_call | solution.py:414
  66.9 0.6 copy.11

commit v10 on v9

--- a/solution.py
+++ b/solution.py
@@ -44,7 +44,7 @@
         py, px = lax.rem(y + dy, side), lax.rem(x + dx, side)
         peers.append((py * side + px, py, px))
     toffsets = [(dz, dc) for dz in range(zn) for dc in range(2) if (dz, dc) != (0, 0)]
-    toffsets.sort(key=lambda o: -(2 * hops(o[0], zn) + o[1]))
+    toffsets.sort(key=lambda o: (-o[1], -hops(o[0], zn)))
     tpeers = [lax.rem(z + dz, zn) * 2 + lax.rem(core + dc, 2) for dz, dc in toffsets]
 
     column = [lax.rem(y + r, side) * side + x for r in range(1, side)]

time: 67.7 us -> 67.6 us (level)
  no operation moved by 1% of the time
where the time goes in v10:
time: 67.6 us; the launch traced here: 67.4 us
  Pallas kernels  66.7 us (99%)
    pallas_call x1, Pallas kernels, shards(): pl.pallas_call(functools.partial(kernel, dims), out_shape=pltpu.VMEM((bat...  66.7 us

profile of v10, /device:TPU:1, one launch (start us, length us, event | category | flops | bytes accessed | tf_op | source)
XLA Modules:
  0.0 67.4 jit_solution(15083170100763116300)
XLA Ops:
  0.0 66.7 %shard_map.91 = f32[8,512]{1,0:T(8,128)S(1)} custom-call(bf16[8,512]{1,0:T(8,128)(2,1)} %hidden_h.1, bf16[4,512]{1,0:T(4,128)(2,1)} %gains_h.1, s32[8]{0:T(128)} %lengths_h.1, bf16[4,512,1024]{2,1,0:T(8,128)(2,1)} %wq_h.1, bf16[4,512,128]{2,1,0:T(8,128)(2,1)} %wk_h.1, bf16[4,512,128]{2,1,0:T(8,128)(2,1)} %wv_h.1, bf16[4,1024,512]{2,1,0:T(8,128)(2,1)} %wo_h.1, ...), custom_call_target="tpu_custom_call" | custom-call | tf_op jit(solution)/shard_map/pallas_call | solution.py:414
  66.8 0.6 copy.11

commit v11 on v9

--- a/solution.py
+++ b/solution.py
@@ -212,8 +212,7 @@
                 square = square + qs[pl.ds(pl.multiple_of(at + 8, 8), 1), :]
             inverse.append(lax.rsqrt(square / total + norm_eps))
             query.append(rounded(rotate(whole * inverse[g], g)))
-        score = [lax.dot_general(
-            query[g].astype(bf16), kb[h, g], (((1,), (1,)), ((), ())), preferred_element_type=f32) for g in both]
+        score = [jnp.dot(query[g].astype(bf16), kb[h, g], preferred_element_type=f32) for g in both]
         new_key = [rounded(rotate(jnp.broadcast_to(fresh_sum[h, 2 * g:2 * g + 1] * inverse[g], (heads, hd)), g)) for g in both]
         new_value = [rounded(fresh_sum[h, 2 * g + 1:2 * g + 2] * inverse[g]) for g in both]
         own = [jnp.sum(query[g] * new_key[g], axis=1, keepdims=True) * scale + own_mask for g in both]
@@ -337,7 +336,7 @@
                 taken(vrv.at[l, h, pl.ds(0, blocks - 2 * h)], hr_sem.at[l, h, 1])
                 for g in range(2):
                     part = slice(g * side, (g + 1) * side)
-                    kb[h, g] = krv[l, h, part].reshape(side * span, hd).astype(bf16)
+                    kb[h, g] = krv[l, h, part].reshape(side * span, hd).T.astype(bf16)
                     vb[h, g] = vrv[l, h, part].reshape(side * span, hd).astype(bf16)
 
             for h in (1, 0):
@@ -432,7 +431,7 @@
             pltpu.VMEM((layers, batch, span, hd), f32),
             pltpu.VMEM((layers, 2, 2 * side, span, hd), f32),
             pltpu.VMEM((layers, 2, 2 * side, span, hd), f32),
-            pltpu.VMEM((2, 2, side * span, hd), bf16),
+            pltpu.VMEM((2, 2, hd, side * span), bf16),
             pltpu.VMEM((2, 2, side * span, hd), bf16),
             pltpu.VMEM((2, n, 3 * heads, hd), f32),
             pltpu.VMEM((2, batch * heads, hd), f32),

time: 67.7 us -> 67.6 us (level)
  no operation moved by 1% of the time
where the time goes in v11:
time: 67.6 us; the launch traced here: 67.4 us
  Pallas kernels  66.8 us (99%)
    pallas_call x1, Pallas kernels, shards(): pl.pallas_call(functools.partial(kernel, dims), out_shape=pltpu.VMEM((bat...  66.8 us

profile of v11, /device:TPU:1, one launch (start us, length us, event | category | flops | bytes accessed | tf_op | source)
XLA Modules:
  0.0 67.4 jit_solution(5496554600872936814)
XLA Ops:
  0.0 66.8 %shard_map.91 = f32[8,512]{1,0:T(8,128)S(1)} custom-call(bf16[8,512]{1,0:T(8,128)(2,1)} %hidden_h.1, bf16[4,512]{1,0:T(4,128)(2,1)} %gains_h.1, s32[8]{0:T(128)} %lengths_h.1, bf16[4,512,1024]{2,1,0:T(8,128)(2,1)} %wq_h.1, bf16[4,512,128]{2,1,0:T(8,128)(2,1)} %wk_h.1, bf16[4,512,128]{2,1,0:T(8,128)(2,1)} %wv_h.1, bf16[4,1024,512]{2,1,0:T(8,128)(2,1)} %wo_h.1, ...), custom_call_target="tpu_custom_call" | custom-call | tf_op jit(solution)/shard_map/pallas_call | solution.py:413
  66.8 0.6 copy.11
